TPU v7x, 128 devices: a whole 4x4x4 slice. The times are simulated.
128 devices in a mesh: layer: 4 (over x), row: 16 (over z, y), col: 2 (over core).
Axes of the slice: x: 4, y: 4, z: 4, core: 2. Of those that a mesh axis runs over, the one named last changes fastest.
Arguments:
- statistic: float32 [8, 7168, 7168], P('layer', 'row', 'col'), as said below
- eigenbasis: float32 [8, 7168, 1024], P('layer', 'col'), may hold values from -0.0625 to 0.0625
Outputs:
- refreshed: float32 [8, 7168, 1024], P('layer', ('row', 'col'))
Inputs may be any that keep to these rules, and one draw needn't show every extreme that they name: `statistic`: each layer's matrix is symmetric and positive definite.
All inputs are finite; a program needn't handle non-finite values.
Results may differ from a plain program's by a relative error of at most 0.00014.
Values sent between devices are 32-bit elements; how exact they have to be, the bound alone decides.
A program may use at most 192 MiB of HBM per device.

v0:
```python
import jax
import jax.numpy as jnp
from jax import lax
from jax.sharding import PartitionSpec as P


def contract(left_operand, right_operand):
    return lax.dot_general(
        left_operand,
        right_operand,
        (((0,), (0,)), ((), ())),
        precision=lax.Precision.HIGHEST,
        preferred_element_type=jnp.float32,
    )


def multiply(left_operand, right_operand):
    return jnp.dot(
        left_operand,
        right_operand,
        precision=lax.Precision.HIGHEST,
        preferred_element_type=jnp.float32,
    )


def on_device(statistic, eigenbasis):
    results = []
    for member in range(statistic.shape[0]):
        stat_layer = statistic[member]
        basis_layer = eigenbasis[member]
        row_product = lax.psum_scatter(
            multiply(stat_layer, basis_layer), "col", scatter_dimension=0, tiled=True
        )
        gram_matrix = lax.psum(contract(row_product, row_product), ("row", "col"))
        factor = jnp.linalg.cholesky(gram_matrix)
        result = lax.linalg.triangular_solve(
            factor, row_product, left_side=False, lower=True, transpose_a=True
        )
        results.append(result)
    return jnp.stack(results)


def solution(mesh):
    placed = (P("layer", "row", "col"), P("layer", "col", None))
    return jax.shard_map(
        on_device,
        mesh=mesh,
        in_specs=placed,
        out_specs=P("layer", ("row", "col"), None),
        check_vma=False,
    )
```

profile of v0, /device:TPU:1, one launch (start us, length us, event | category | flops | bytes accessed | tf_op | source)
XLA Modules:
  0.0 879.6 jit_solution(4756116928525177260)
XLA Ops:
  6.5 25.2 %fusion.2 = f32[448,1024]{1,0:T(8,128)} fusion(f32[2,3584,1024]{2,1,0:T(8,128)} %param.6, f32[2,448,3584]{2,1,0:T(8,128)} %param.5), kind=kOutput, calls=%fused_computation.6 | convolution fusion | flops 19730006016 | bytes 22937600 | tf_op jit(solution)/shard_map/dot_general | solution.py:18
  31.8 25.2 %fusion = f32[448,1024]{1,0:T(8,128)} fusion(f32[2,3584,1024]{2,1,0:T(8,128)} %param.6, f32[2,448,3584]{2,1,0:T(8,128)} %param.5), kind=kOutput, calls=%fused_computation.4 | convolution fusion | flops 19730006016 | bytes 22937600 | tf_op jit(solution)/shard_map/dot_general | solution.py:18
  57.2 6.9 fusion.134
  64.2 8.6 reduce-scatter.5.cloned.1.call-done
  72.7 7.1 fusion.135
  79.9 121.7 %all-reduce.4.cloned.1.call-done = (f32[1024,1024]{0,1:T(8,128)}, f32[1024,1024]{0,1:T(8,128)}) async-done(((f32[1024,1024]{0,1:T(8,128)}, f32[1024,1024]{0,1:T(8,128)}), (f32[1024,1024]{0,1:T(8,128)}, f32[1024,1024]{0,1:T(8,128)})) %all-reduce.4.cloned.1.call-update) | async-done | bytes 8388624 | tf_op jit(solution)/shard_map/psum | solution.py:34
  201.6 5.3 copy.4
  206.9 5.6 copy.6
  212.5 10.3 %fusion.10 = (f32[1024,1024]{1,0:T(8,128)}, f32[1024,1024]{1,0:T(8,128)S(1)}) fusion(f32[1024,1024]{1,0:T(8,128)} %copy.6, f32[1024,1024]{0,1:T(8,128)} %get-tuple-element.39, f32[1024,1024]{1,0:T(8,128)} %copy.4, f32[1024,1024]{0,1:T(8,128)} %get-tuple-element.40), kind=kLoop, calls=%fused_computation.17 | loop fusion | flops 4194304 | bytes 25165824 | tf_op jit(solution)/shard_map/jit(cholesky)/div | solution.py:35
  224.8 11.7 %cholesky.619 = f32[128,128]{1,0:T(8,128)S(1)} custom-call(f32[128,128]{1,0:T(8,128)S(1)} %cholesky.911), custom_call_target="Cholesky" | custom-call | tf_op jit(solution)/shard_map/jit(cholesky)/cholesky | solution.py:35
  236.5 9.8 %custom-call.55 = f32[1,128,128]{1,2,0:T(8,128)S(1)} custom-call(f32[1,128,128]{2,1,0:T(8,128)S(1)} %get-tuple-element.116), custom_call_target="InvertDiagBlocksLowerTriangular" | custom-call | tf_op jit(solution)/shard_map/jit(cholesky)/cholesky | solution.py:35
  246.3 2.5 cholesky.645
  248.8 2.4 constant_dynamic-update-slice_fusion.63
  252.8 12.1 %cholesky.638 = f32[128,128]{1,0:T(8,128)S(1)} custom-call(f32[128,128]{1,0:T(8,128)S(1)} %cholesky.915), custom_call_target="Cholesky" | custom-call | tf_op jit(solution)/shard_map/jit(cholesky)/cholesky | solution.py:35
  266.8 9.8 %custom-call.56 = f32[1,128,128]{1,2,0:T(8,128)S(1)} custom-call(f32[1,128,128]{2,1,0:T(8,128)S(1)} %get-tuple-element.113), custom_call_target="InvertDiagBlocksLowerTriangular" | custom-call | tf_op jit(solution)/shard_map/jit(cholesky)/cholesky | solution.py:35
  279.9 11.7 %cholesky.659 = f32[128,128]{1,0:T(8,128)S(1)} custom-call(f32[128,128]{1,0:T(8,128)S(1)} %cholesky.920), custom_call_target="Cholesky" | custom-call | tf_op jit(solution)/shard_map/jit(cholesky)/cholesky | solution.py:35
  292.9 9.8 %custom-call.57 = f32[1,128,128]{1,2,0:T(8,128)S(1)} custom-call(f32[1,128,128]{2,1,0:T(8,128)S(1)} %get-tuple-element.110), custom_call_target="InvertDiagBlocksLowerTriangular" | custom-call | tf_op jit(solution)/shard_map/jit(cholesky)/cholesky | solution.py:35
  303.9 2.5 convolution_subtract_fusion.5
  306.4 11.7 %cholesky.678 = f32[128,128]{1,0:T(8,128)S(1)} custom-call(f32[128,128]{1,0:T(8,128)S(1)} %cholesky.925), custom_call_target="Cholesky" | custom-call | tf_op jit(solution)/shard_map/jit(cholesky)/cholesky | solution.py:35
  319.4 9.8 %custom-call.58 = f32[1,128,128]{1,2,0:T(8,128)S(1)} custom-call(f32[1,128,128]{2,1,0:T(8,128)S(1)} %get-tuple-element.107), custom_call_target="InvertDiagBlocksLowerTriangular" | custom-call | tf_op jit(solution)/shard_map/jit(cholesky)/cholesky | solution.py:35
  330.3 2.3 convolution_subtract_fusion.7
  332.7 11.7 %cholesky.697 = f32[128,128]{1,0:T(8,128)S(1)} custom-call(f32[128,128]{1,0:T(8,128)S(1)} %cholesky.930), custom_call_target="Cholesky" | custom-call | tf_op jit(solution)/shard_map/jit(cholesky)/cholesky | solution.py:35
  345.7 10.0 %custom-call.59 = f32[1,128,128]{1,2,0:T(8,128)S(1)} custom-call(f32[1,128,128]{2,1,0:T(8,128)S(1)} %get-tuple-element.104), custom_call_target="InvertDiagBlocksLowerTriangular" | custom-call | tf_op jit(solution)/shard_map/jit(cholesky)/cholesky | solution.py:35
  356.7 2.3 convolution_subtract_fusion.9
  359.0 11.7 %cholesky.716 = f32[128,128]{1,0:T(8,128)S(1)} custom-call(f32[128,128]{1,0:T(8,128)S(1)} %cholesky.935), custom_call_target="Cholesky" | custom-call | tf_op jit(solution)/shard_map/jit(cholesky)/cholesky | solution.py:35
  372.0 9.8 %custom-call.60 = f32[1,128,128]{1,2,0:T(8,128)S(1)} custom-call(f32[1,128,128]{2,1,0:T(8,128)S(1)} %get-tuple-element.101), custom_call_target="InvertDiagBlocksLowerTriangular" | custom-call | tf_op jit(solution)/shard_map/jit(cholesky)/cholesky | solution.py:35
  384.8 12.1 %cholesky.735 = f32[128,128]{1,0:T(8,128)S(1)} custom-call(f32[128,128]{1,0:T(8,128)S(1)} %cholesky.940), custom_call_target="Cholesky" | custom-call | tf_op jit(solution)/shard_map/jit(cholesky)/cholesky | solution.py:35
  398.3 9.8 %custom-call.61 = f32[1,128,128]{1,2,0:T(8,128)S(1)} custom-call(f32[1,128,128]{2,1,0:T(8,128)S(1)} %get-tuple-element.98), custom_call_target="InvertDiagBlocksLowerTriangular" | custom-call | tf_op jit(solution)/shard_map/jit(cholesky)/cholesky | solution.py:35
  410.7 11.7 %cholesky.752 = f32[128,128]{1,0:T(8,128)S(1)} custom-call(f32[128,128]{1,0:T(8,128)S(1)} %convolution_subtract_fusion.27), custom_call_target="Cholesky" | custom-call | tf_op jit(solution)/shard_map/jit(cholesky)/cholesky | solution.py:35
  428.6 4.8 select_select_fusion.1
  433.4 22.8 %while.4 = (s32[]{:T(128)}, f32[1024,1024]{1,0:T(8,128)}, s32[8,2]{0,1:T(2,128)S(1)}, f32[8,128,128]{2,1,0:T(8,128)S(1)}, s32[]{:T(128)}) while((s32[]{:T(128)}, f32[1024,1024]{1,0:T(8,128)}, s32[8,2]{0,1:T(2,128)S(1)}, f32[8,128,128]{2,1,0:T(8,128)S(1)}, s32[]{:T(128)}) %tuple.114), condition=%wide.while_cond, body=%wide.while_body.sunk | while | flops 2 | bytes 131181 | solution.py:36
  434.1 2.2 bitcast_dynamic-update-slice_fusion.4
  436.9 2.2 bitcast_dynamic-update-slice_fusion.4
  439.8 2.2 bitcast_dynamic-update-slice_fusion.4
  442.7 2.2 bitcast_dynamic-update-slice_fusion.4
  445.5 2.2 bitcast_dynamic-update-slice_fusion.4
  448.4 2.2 bitcast_dynamic-update-slice_fusion.4
  451.2 2.2 bitcast_dynamic-update-slice_fusion.4
  456.3 78.8 %custom-call.62 = f32[8,128,128]{1,2,0:T(8,128)S(1)} custom-call(f32[8,128,128]{2,1,0:T(8,128)S(1)} %get-tuple-element.21), custom_call_target="InvertDiagBlocksLowerTriangular" | custom-call | tf_op jit(solution)/shard_map/triangular_solve/custom-call.7 | solution.py:36
  535.9 11.7 %cholesky.767 = f32[128,128]{1,0:T(8,128)S(1)} custom-call(f32[128,128]{1,0:T(8,128)S(1)} %cholesky.944), custom_call_target="Cholesky" | custom-call | tf_op jit(solution)/shard_map/jit(cholesky)/cholesky | solution.py:35
  547.6 9.8 %custom-call.63 = f32[1,128,128]{1,2,0:T(8,128)S(1)} custom-call(f32[1,128,128]{2,1,0:T(8,128)S(1)} %get-tuple-element.138), custom_call_target="InvertDiagBlocksLowerTriangular" | custom-call | tf_op jit(solution)/shard_map/jit(cholesky)/cholesky | solution.py:35
  557.5 2.5 cholesky.793
  560.0 2.3 constant_dynamic-update-slice_fusion.61
  563.9 11.7 %cholesky.786 = f32[128,128]{1,0:T(8,128)S(1)} custom-call(f32[128,128]{1,0:T(8,128)S(1)} %cholesky.948), custom_call_target="Cholesky" | custom-call | tf_op jit(solution)/shard_map/jit(cholesky)/cholesky | solution.py:35
  577.5 10.0 %custom-call.64 = f32[1,128,128]{1,2,0:T(8,128)S(1)} custom-call(f32[1,128,128]{2,1,0:T(8,128)S(1)} %get-tuple-element.135), custom_call_target="InvertDiagBlocksLowerTriangular" | custom-call | tf_op jit(solution)/shard_map/jit(cholesky)/cholesky | solution.py:35
  590.9 11.7 %cholesky.807 = f32[128,128]{1,0:T(8,128)S(1)} custom-call(f32[128,128]{1,0:T(8,128)S(1)} %cholesky.953), custom_call_target="Cholesky" | custom-call | tf_op jit(solution)/shard_map/jit(cholesky)/cholesky | solution.py:35
  604.0 9.8 %custom-call.65 = f32[1,128,128]{1,2,0:T(8,128)S(1)} custom-call(f32[1,128,128]{2,1,0:T(8,128)S(1)} %get-tuple-element.132), custom_call_target="InvertDiagBlocksLowerTriangular" | custom-call | tf_op jit(solution)/shard_map/jit(cholesky)/cholesky | solution.py:35
  615.0 2.3 convolution_subtract_fusion.4
  617.3 12.1 %cholesky.826 = f32[128,128]{1,0:T(8,128)S(1)} custom-call(f32[128,128]{1,0:T(8,128)S(1)} %cholesky.958), custom_call_target="Cholesky" | custom-call | tf_op jit(solution)/shard_map/jit(cholesky)/cholesky | solution.py:35
  630.7 9.8 %custom-call.66 = f32[1,128,128]{1,2,0:T(8,128)S(1)} custom-call(f32[1,128,128]{2,1,0:T(8,128)S(1)} %get-tuple-element.129), custom_call_target="InvertDiagBlocksLowerTriangular" | custom-call | tf_op jit(solution)/shard_map/jit(cholesky)/cholesky | solution.py:35
  641.6 2.3 convolution_subtract_fusion.6
  643.9 11.7 %cholesky.845 = f32[128,128]{1,0:T(8,128)S(1)} custom-call(f32[128,128]{1,0:T(8,128)S(1)} %cholesky.963), custom_call_target="Cholesky" | custom-call | tf_op jit(solution)/shard_map/jit(cholesky)/cholesky | solution.py:35
  656.9 9.8 %custom-call.67 = f32[1,128,128]{1,2,0:T(8,128)S(1)} custom-call(f32[1,128,128]{2,1,0:T(8,128)S(1)} %get-tuple-element.126), custom_call_target="InvertDiagBlocksLowerTriangular" | custom-call | tf_op jit(solution)/shard_map/jit(cholesky)/cholesky | solution.py:35
  667.8 2.5 convolution_subtract_fusion.8
  670.3 11.7 %cholesky.864 = f32[128,128]{1,0:T(8,128)S(1)} custom-call(f32[128,128]{1,0:T(8,128)S(1)} %cholesky.968), custom_call_target="Cholesky" | custom-call | tf_op jit(solution)/shard_map/jit(cholesky)/cholesky | solution.py:35
  683.3 9.8 %custom-call.68 = f32[1,128,128]{1,2,0:T(8,128)S(1)} custom-call(f32[1,128,128]{2,1,0:T(8,128)S(1)} %get-tuple-element.123), custom_call_target="InvertDiagBlocksLowerTriangular" | custom-call | tf_op jit(solution)/shard_map/jit(cholesky)/cholesky | solution.py:35
  696.2 11.7 %cholesky.883 = f32[128,128]{1,0:T(8,128)S(1)} custom-call(f32[128,128]{1,0:T(8,128)S(1)} %cholesky.973), custom_call_target="Cholesky" | custom-call | tf_op jit(solution)/shard_map/jit(cholesky)/cholesky | solution.py:35
  709.2 10.0 %custom-call.69 = f32[1,128,128]{1,2,0:T(8,128)S(1)} custom-call(f32[1,128,128]{2,1,0:T(8,128)S(1)} %get-tuple-element.120), custom_call_target="InvertDiagBlocksLowerTriangular" | custom-call | tf_op jit(solution)/shard_map/jit(cholesky)/cholesky | solution.py:35
  721.8 11.7 %cholesky.900 = f32[128,128]{1,0:T(8,128)S(1)} custom-call(f32[128,128]{1,0:T(8,128)S(1)} %convolution_subtract_fusion.26), custom_call_target="Cholesky" | custom-call | tf_op jit(solution)/shard_map/jit(cholesky)/cholesky | solution.py:35
  739.7 4.9 select_select_fusion
  744.7 22.5 %while.5 = (s32[]{:T(128)}, f32[1024,1024]{1,0:T(8,128)}, s32[8,2]{0,1:T(2,128)S(1)}, f32[8,128,128]{2,1,0:T(8,128)S(1)}, s32[]{:T(128)}) while((s32[]{:T(128)}, f32[1024,1024]{1,0:T(8,128)}, s32[8,2]{0,1:T(2,128)S(1)}, f32[8,128,128]{2,1,0:T(8,128)S(1)}, s32[]{:T(128)}) %tuple.124), condition=%wide.while_cond.clone, body=%wide.while_body.clone.sunk | while | flops 2 | bytes 131181 | solution.py:36
  745.3 2.2 bitcast_dynamic-update-slice_fusion.5
  748.1 2.2 bitcast_dynamic-update-slice_fusion.5
  767.2 78.8 %custom-call.70 = f32[8,128,128]{1,2,0:T(8,128)S(1)} custom-call(f32[8,128,128]{2,1,0:T(8,128)S(1)} %get-tuple-element.22), custom_call_target="InvertDiagBlocksLowerTriangular" | custom-call | tf_op jit(solution)/shard_map/triangular_solve/custom-call.7 | solution.py:36
  (153 shorter events, 101.8 us)
Async XLA Ops:
  6.5 50.7 %reduce-scatter.3.cloned.1.call-start = ((), (), s32[]{:S(2)}) async-start(), calls=%async_computation.2 | async-start | bytes 2752512 | tf_op jit(solution)/shard_map/reduce_scatter | solution.py:31
  31.7 41.0 %reduce-scatter.5.cloned.1.call-start = ((), (), s32[]{:S(2)}) async-start(), calls=%async_computation.3 | async-start | bytes 2752512 | tf_op jit(solution)/shard_map/reduce_scatter | solution.py:31
  57.0 144.6 %all-reduce.4.cloned.1.call-start = ((), (), s32[]{:S(2)}) async-start(), calls=%async_computation.4 | async-start | bytes 16777216 | tf_op jit(solution)/shard_map/psum | solution.py:34
  222.8 1.9 copy-start.2
  739.7 106.3 %copy-start.1 = (f32[224,1024]{1,0:T(8,128)S(1)}, f32[224,1024]{1,0:T(8,128)}, u32[]{:S(2)}) copy-start(f32[224,1024]{1,0:T(8,128)} %reduce-scatter.3.cloned.1.call-done) | copy-start | bytes 2752516
  849.2 9.4 %copy-start = (f32[224,1024]{1,0:T(8,128)S(1)}, f32[224,1024]{1,0:T(8,128)}, u32[]{:S(2)}) copy-start(f32[224,1024]{1,0:T(8,128)} %reduce-scatter.5.cloned.1.call-done) | copy-start | bytes 2752516
Sparse Core Ops, SparseCore 0:
  31.9 15.5 reduce-scatter.2
  57.1 15.5 reduce-scatter.4
  80.0 121.5 all-reduce.3
where the time goes:
time: 888 us; the launch traced here: 880 us
  other arithmetic  525 us (59%)
  matrix products  136 us (15%)
  waiting for transfers between devices  130 us (15%)
  local copies, waits for them, and re-layouts  63.8 us (7%)
  between operations  24 us (3%)
    another operation x62, other arithmetic, on_device(): factor = jnp.linalg.cholesky(gram_matrix)  346 us
    another operation x5, other arithmetic, on_device(): lax.linalg.triangular_solve(factor, row_product, left_side=False, lower=T...  167 us
    psum x1, waiting for transfers between devices, on_device(): gram_matrix = lax.psum(contract(row_product, row_product), ('row', 'col'))  122 us
    dot_general x2, matrix products, multiply(): jnp.dot(left_operand, right_operand, precision=lax.Precision.HIGHEST, pre...  50.3 us
    another operation x28, matrix products, on_device(): factor = jnp.linalg.cholesky(gram_matrix)  46.5 us
    another operation x51, local copies, waits for them, and re-layouts, on_device(): lax.linalg.triangular_solve(factor, row_product, left_side=False, lower=T...  45.1 us
    another operation x30, matrix products, on_device(): lax.linalg.triangular_solve(factor, row_product, left_side=False, lower=T...  24.9 us
  transfers between devices with their start and end apart: 3, of which 2 were waited for; matrix products, arithmetic and copies ran while one was open for 4% of the time, Pallas kernels for 0%

commit v1 on v0

v1 whole, which is shorter than its diff:
```python
import functools
import jax, jax.numpy as jnp
from jax import lax
from jax.experimental import pallas as pl
from jax.experimental.pallas import tpu as pltpu
from jax.sharding import PartitionSpec as P

F32, BF16 = jnp.float32, jnp.bfloat16

def halves(x):
    hi = x.astype(BF16)
    lo = (x - hi.astype(F32)).astype(BF16)
    return hi, lo

def left_stack(x):
    hi, lo = halves(x)
    return jnp.concatenate([hi, lo, hi, lo], axis=1)

def right_stack(x):
    hi, lo = halves(x)
    return jnp.concatenate([hi, hi, lo, lo], axis=0)

def dot(a, b):
    return jnp.dot(a, b, preferred_element_type=F32)

def factor_group(rows, inv, col0):
    n = len(rows)
    sub = lax.broadcasted_iota(jnp.int32, (8, 128), 0)
    for t in range(n):
        base = col0 + 8 * t
        cols = [[jnp.broadcast_to(rows[g][:, base + j:base + j + 1], (8, 128)) for g in range(t, n)] for j in range(8)]
        scale = None
        for j in range(8):
            pivot = jnp.broadcast_to(cols[j][0][j:j + 1, :], (8, 128))
            recip = 1.0 / pivot
            rs = lax.rsqrt(pivot)
            scale = rs if scale is None else jnp.where(sub >= j, rs, scale)
            mult = [c * recip for c in cols[j]]
            mult[0] = jnp.where(sub > j, mult[0], 0.0)
            for k in range(j + 1, 8):
                across = jnp.broadcast_to(cols[k][0][j:j + 1, :], (8, 128))
                cols[k] = [c - m * across for c, m in zip(cols[k], mult)]
            row = jnp.broadcast_to(rows[t][j:j + 1, :], (8, 128))
            irow = jnp.broadcast_to(inv[t][j:j + 1, :], (8, 128))
            for g in range(t, n):
                rows[g] = rows[g] - mult[g - t] * row
                inv[g] = inv[g] - mult[g - t] * irow
        rows[t] = rows[t] * scale
        inv[t] = inv[t] * scale
    return rows, inv

def diag_inverse(load, work, winv):
    r = lax.broadcasted_iota(jnp.int32, (128, 128), 0)
    c = lax.broadcasted_iota(jnp.int32, (128, 128), 1)
    work[...] = load
    winv[...] = jnp.where(r == c, 1.0, 0.0).astype(F32)
    step = 32
    for q in range(128 // step):
        lo = q * step
        rows = [work[lo + 8 * g:lo + 8 * g + 8, :] for g in range(step // 8)]
        inv = [winv[lo + 8 * g:lo + 8 * g + 8, :] for g in range(step // 8)]
        rows, inv = factor_group(rows, inv, lo)
        rfull = jnp.concatenate(rows, axis=0)
        ifull = jnp.concatenate(inv, axis=0)
        winv[lo:lo + step, :] = ifull
        if lo + step < 128:
            both = right_stack(jnp.concatenate([rfull, ifull], axis=1))
            lt = left_stack(rfull.T)
            upd = dot(lt[lo + step:, :], both)
            work[lo + step:, :] -= upd[:, :128]
            winv[lo + step:, :] -= upd[:, 128:]

def kernel(n, g_ref, p_ref, x_ref, G, work, winv, Rr):
    G[...] = g_ref[...]
    x_ref[...] = p_ref[...]

    def body(k, carry):
        at = pl.multiple_of(k * 128, 128)
        diag_inverse(G[pl.ds(at, 128), pl.ds(at, 128)], work, winv)
        m = winv[...]
        ml = left_stack(m)
        mt = right_stack(m.T)
        for kk in range(n):
            @pl.when(k == kk)
            def _():
                a = kk * 128
                b = a + 128
                xk = dot(left_stack(x_ref[:, a:b]), mt)
                x_ref[:, a:b] = xk
                if kk < n - 1:
                    r = dot(ml, right_stack(G[a:b, b:]))
                    rr = right_stack(r)
                    x_ref[:, b:] -= dot(left_stack(xk), rr)
                    w = n * 128 - b
                    for i in range(0, w, 256):
                        e = min(i + 256, w)
                        lt = left_stack(r[:, i:e].T)
                        G[b + i:b + e, b + i:] -= dot(lt, rr[:, i:])
        return carry
    lax.fori_loop(0, n, body, 0)

def chol_solve(gram, prod):
    k = gram.shape[0]
    n = k // 128
    vm = pl.BlockSpec(memory_space=pltpu.VMEM)
    return pl.pallas_call(
        functools.partial(kernel, n),
        out_shape=jax.ShapeDtypeStruct(prod.shape, F32),
        in_specs=[vm, vm],
        out_specs=vm,
        scratch_shapes=[pltpu.VMEM((k, k), F32), pltpu.VMEM((128, 128), F32), pltpu.VMEM((128, 128), F32), pltpu.VMEM((8, 128), F32)],
        compiler_params=pltpu.CompilerParams(vmem_limit_bytes=48 << 20),
        name="chol_solve",
    )(gram, prod)


HIGH = lax.Precision.HIGH


def on_device(statistic, eigenbasis):
    partial = jnp.stack(
        [jnp.dot(statistic[l], eigenbasis[l], precision=HIGH, preferred_element_type=F32) for l in range(2)]
    )
    product = lax.psum_scatter(partial, "col", scatter_dimension=0, tiled=False)
    gram = lax.dot_general(product, product, (((0,), (0,)), ((), ())), precision=HIGH, preferred_element_type=F32)
    gram = lax.psum(gram, "row")
    x = chol_solve(gram, product)
    x = x.reshape(2, x.shape[0] // 2, x.shape[1])
    return lax.all_to_all(x, "col", 0, 0)


def solution(mesh):
    placed = (P("layer", "row", "col"), P("layer", "col", None))
    return jax.shard_map(
        on_device,
        mesh=mesh,
        in_specs=placed,
        out_specs=P("layer", ("row", "col"), None),
        check_vma=False,
    )
```

time: 888 us -> 226 us (0.25)
  other arithmetic: 525 us -> 2.05 us
  matrix products: 136 us -> 37.1 us
  local copies, waits for them, and re-layouts: 63.8 us -> 1.24 us
  Pallas kernels: 0 us -> 42.8 us
  between operations: 24 us -> 13.4 us
    another operation x68 -> x1, other arithmetic: 515 us -> 2.05 us  [on_device(): jnp.stack([jnp.dot(statistic[l], eigenbasis[l], precision=HIGH, preferred...]
    another operation x58 -> x0, matrix products: 71.4 us -> none  [the longest x28 46.5 us: on_device(): factor = jnp.linalg.cholesky(gram_matrix)]
    another operation x67 -> x0, local copies, waits for them, and re-layouts: 51 us -> none  [the longest x51 45.1 us: on_device(): lax.linalg.triangular_solve(factor, row_product, left_side=False, lower=T...]
    pallas_call x0 -> x1, Pallas kernels: none -> 42.8 us  [chol_solve(): pl.pallas_call(functools.partial(kernel, n), out_shape=jax.ShapeDtypeStru...]
    dot_general x4 -> x3, matrix products: 64.4 us -> 37.1 us  [the longest x2 29.4 us: on_device(): jnp.dot(statistic[l], eigenbasis[l], precision=HIGH, preferred_element_ty...]
    psum x1, waiting for transfers between devices: 122 us -> 105 us  [on_device(): gram = lax.psum(gram, 'row')]
    psum x2 -> x0, local copies, waits for them, and re-layouts: 10.9 us -> none  [on_device(): gram_matrix = lax.psum(contract(row_product, row_product), ('row', 'col'))]
    div x1 -> x0, other arithmetic: 10.3 us -> none  [on_device(): factor = jnp.linalg.cholesky(gram_matrix)]
  transfers between devices with their start and end apart: 3 -> 2, of which waited for: 2 -> 2; matrix products, arithmetic and copies ran while one was open for 4% -> 0% of each run, Pallas kernels for 0% -> 0%
where the time goes in v1:
time: 226 us
  waiting for transfers between devices  123 us (54%)
  Pallas kernels  42.8 us (19%)
  matrix products  37.1 us (16%)
  between operations  13.4 us (6%)
  blocking collectives  5.99 us (3%)
    psum x1, waiting for transfers between devices, on_device(): gram = lax.psum(gram, 'row')  105 us
    pallas_call x1, Pallas kernels, chol_solve(): pl.pallas_call(functools.partial(kernel, n), out_shape=jax.ShapeDtypeStru...  42.8 us
    dot_general x2, matrix products, on_device(): jnp.dot(statistic[l], eigenbasis[l], precision=HIGH, preferred_element_ty...  29.4 us
    reduce_scatter x1, waiting for transfers between devices, on_device(): product = lax.psum_scatter(partial, 'col', scatter_dimension=0, tiled=False)  18 us
    dot_general x1, matrix products, on_device(): lax.dot_general(product, product, (((0,), (0,)), ((), ())), precision=HIG...  7.67 us
    all_to_all x1, blocking collectives, on_device(): return lax.all_to_all(x, 'col', 0, 0)  5.99 us
  transfers between devices with their start and end apart: 2, of which 2 were waited for; matrix products, arithmetic and copies ran while one was open for 0% of the time, Pallas kernels for 0%

profile of v1, /device:TPU:1, one launch (start us, length us, event | category | flops | bytes accessed | tf_op | source)
XLA Modules:
  0.0 225.5 jit_solution(16350261882991432377)
XLA Ops:
  6.5 0.0 reduce-scatter.2.cloned.1.call-start
  6.5 0.0 copy-start.1
  6.5 15.2 %fusion.15 = f32[1,448,1024]{2,1,0:T(8,128)S(1)} fusion(f32[2,3584,1024]{2,1,0:T(8,128)} %param.3, f32[2,448,3584]{2,1,0:T(8,128)} %param.2), kind=kOutput, calls=%fused_computation.12 | convolution fusion | flops 9865003008 | bytes 22937600 | tf_op jit(solution)/shard_map/dot_general | solution.py:122
  21.8 0.0 copy-done.1
  21.8 14.2 %fusion.10 = f32[1,448,1024]{2,1,0:T(8,128)S(1)} fusion(f32[2,3584,1024]{2,1,0:T(8,128)} %param.3, f32[2,448,3584]{2,1,0:T(8,128)S(1)} %copy-done.1), kind=kOutput, calls=%fused_computation.11 | convolution fusion | flops 9865003008 | bytes 22937600 | tf_op jit(solution)/shard_map/dot_general | solution.py:122
  36.0 2.1 pad_maximum_fusion
  38.0 0.0 reduce-scatter.2.cloned.1.call-update
  38.1 0.2 all-reduce.2.cloned.1.call-start
  38.3 18.0 %reduce-scatter.2.cloned.1.call-done = f32[1,448,1024]{2,1,0:T(8,128)} async-done(((f32[2,448,1024]{2,1,0:T(8,128)}), f32[1,448,1024]{2,1,0:T(8,128)}) %reduce-scatter.2.cloned.1.call-update) | async-done | bytes 1835024 | tf_op jit(solution)/shard_map/reduce_scatter | solution.py:124
  56.3 0.0 copy-start
  56.3 7.7 %fusion.20 = f32[1024,1024]{1,0:T(8,128)} fusion(f32[1,448,1024]{2,1,0:T(8,128)} %reduce-scatter.2.cloned.1.call-done), kind=kOutput, calls=%fused_computation.13 | convolution fusion | flops 2818572288 | bytes 6029312 | tf_op jit(solution)/shard_map/dot_general | solution.py:125
  64.0 0.0 all-reduce.2.cloned.1.call-update
  64.0 104.7 %all-reduce.2.cloned.1.call-done.g_ref = f32[1024,1024]{1,0:T(8,128)} async-done(((f32[1024,1024]{1,0:T(8,128)}), f32[1024,1024]{1,0:T(8,128)}) %all-reduce.2.cloned.1.call-update) | async-done | bytes 4194320 | tf_op jit(solution)/shard_map/psum | solution.py:126
  168.7 0.0 copy-done
  168.7 42.8 %chol_solve.1 = f32[448,1024]{1,0:T(8,128)S(1)} custom-call(f32[1024,1024]{1,0:T(8,128)} %all-reduce.2.cloned.1.call-done.g_ref, f32[448,1024]{1,0:T(8,128)S(1)} %bitcast.29), custom_call_target="tpu_custom_call" | custom-call | tf_op jit(solution)/shard_map/chol_solve/pallas_call | solution.py:106
  211.5 6.0 %all_to_all.5 = f32[2,224,1024]{2,1,0:T(8,128)S(1)} all-to-all(f32[2,224,1024]{2,1,0:T(8,128)S(1)} %bitcast.28), channel_id=1, replica_groups=mesh['layer'=4,'row'=16,'col'=2] {'col'}, dimensions={0} | all-to-all | bytes 3670016 | tf_op jit(solution)/shard_map/all_to_all | solution.py:129
  217.4 1.2 copy.5
Async XLA Ops:
  6.5 49.8 %reduce-scatter.2.cloned.1.call-start = ((), (), s32[]{:S(2)}) async-start(), calls=%async_computation.2 | async-start | bytes 5505024 | tf_op jit(solution)/shard_map/reduce_scatter | solution.py:124
  6.5 15.2 %copy-start.1 = (f32[2,448,3584]{2,1,0:T(8,128)S(1)}, f32[2,448,3584]{2,1,0:T(8,128)}, u32[]{:S(2)}) copy-start(f32[2,448,3584]{2,1,0:T(8,128)} %param.2) | copy-start | bytes 38535172
  38.1 130.6 %all-reduce.2.cloned.1.call-start = ((), (), s32[]{:S(2)}) async-start(), calls=%async_computation.3 | async-start | bytes 8388608 | tf_op jit(solution)/shard_map/psum | solution.py:126
  56.3 112.4 %copy-start = (f32[1,448,1024]{2,1,0:T(8,128)S(1)}, f32[1,448,1024]{2,1,0:T(8,128)}, u32[]{:S(2)}) copy-start(f32[1,448,1024]{2,1,0:T(8,128)} %reduce-scatter.2.cloned.1.call-done) | copy-start | bytes 5505028
Sparse Core Ops, SparseCore 0:
  38.2 18.0 reduce-scatter.1
  64.1 104.4 all-reduce.1

commit v2 on v0

v2 whole, which is shorter than its diff:
```python
import functools
import jax
import jax.numpy as jnp
from jax import lax
from jax.experimental import pallas as pl
from jax.experimental.pallas import tpu as pltpu
from jax.sharding import PartitionSpec as P

F32, BF16 = jnp.float32, jnp.bfloat16
MESH = pl.DeviceIdType.MESH
HIGH = lax.Precision.HIGH
B = 128


def halves(x):
    hi = x.astype(BF16)
    lo = (x - hi.astype(F32)).astype(BF16)
    return hi, lo


def dot(a, b):
    return jnp.dot(a, b, preferred_element_type=F32)


def dot_t(a, b):
    return lax.dot_general(a, b, (((1,), (1,)), ((), ())), preferred_element_type=F32)


def left_stack(x):
    hi, lo = halves(x)
    return jnp.concatenate([hi, lo, hi, lo], axis=1)


def right_stack(x):
    hi, lo = halves(x)
    return jnp.concatenate([hi, hi, lo, lo], axis=0)


def factor_group(rows, inv, col0):
    n = len(rows)
    sub = lax.broadcasted_iota(jnp.int32, (8, 128), 0)
    for t in range(n):
        base = col0 + 8 * t
        cols = [
            [jnp.broadcast_to(rows[g][:, base + j : base + j + 1], (8, 128)) for g in range(t, n)]
            for j in range(8)
        ]
        scale = None
        for j in range(8):
            pivot = jnp.broadcast_to(cols[j][0][j : j + 1, :], (8, 128))
            recip = 1.0 / pivot
            rs = lax.rsqrt(pivot)
            scale = rs if scale is None else jnp.where(sub >= j, rs, scale)
            mult = [c * recip for c in cols[j]]
            mult[0] = jnp.where(sub > j, mult[0], 0.0)
            for k in range(j + 1, 8):
                across = jnp.broadcast_to(cols[k][0][j : j + 1, :], (8, 128))
                cols[k] = [c - m * across for c, m in zip(cols[k], mult)]
            row = jnp.broadcast_to(rows[t][j : j + 1, :], (8, 128))
            irow = jnp.broadcast_to(inv[t][j : j + 1, :], (8, 128))
            for g in range(t, n):
                rows[g] = rows[g] - mult[g - t] * row
                inv[g] = inv[g] - mult[g - t] * irow
        rows[t] = rows[t] * scale
        inv[t] = inv[t] * scale
    return rows, inv


def diag_inverse(block, work, winv):
    r = lax.broadcasted_iota(jnp.int32, (B, B), 0)
    c = lax.broadcasted_iota(jnp.int32, (B, B), 1)
    work[...] = block
    winv[...] = jnp.where(r == c, 1.0, 0.0).astype(F32)
    step = 32
    for q in range(B // step):
        lo = q * step
        rows = [work[lo + 8 * g : lo + 8 * g + 8, :] for g in range(step // 8)]
        inv = [winv[lo + 8 * g : lo + 8 * g + 8, :] for g in range(step // 8)]
        rows, inv = factor_group(rows, inv, lo)
        rfull = jnp.concatenate(rows, axis=0)
        ifull = jnp.concatenate(inv, axis=0)
        winv[lo : lo + step, :] = ifull
        if lo + step < B:
            both = right_stack(jnp.concatenate([rfull, ifull], axis=1))
            lt = left_stack(rfull.T)
            upd = dot(lt[lo + step :, :], both)
            work[lo + step :, :] -= upd[:, :B]
            winv[lo + step :, :] -= upd[:, B:]
    return winv[...]


def panel_at(k):
    return B * k * (k + 1) // 2


def kernel(nb, part, out, pin, phi, plo, thi, tlo, gloc, gfull, ysum, r1, r2, whi, wlo, x, work, winv,
           xsend, xrecv, osend, orecv, asend, arecv):
    core = lax.axis_index("col")
    row = lax.axis_index("row")
    a, b = row // 4, row % 4
    mate = {"col": 1 - core}

    def along(first, d):
        if first:
            return a * 4 + (b + d) % 4
        return ((a + d) % 4) * 4 + b

    barrier = pltpu.get_barrier_semaphore()
    pl.semaphore_signal(barrier, inc=1, device_id=mate, device_id_type=MESH)
    for d in range(1, 4):
        pl.semaphore_signal(barrier, inc=1, device_id={"row": along(True, d)}, device_id_type=MESH)
        pl.semaphore_signal(barrier, inc=1, device_id={"row": along(False, d)}, device_id_type=MESH)
    pl.semaphore_wait(barrier, 7)

    rows = phi.shape[0]
    half = rows // 2
    sends = []

    def swap(q):
        cols = slice(256 * q, 256 * q + 256)
        return pltpu.make_async_remote_copy(
            src_ref=part.at[1 - core, :, cols], dst_ref=pin.at[:, cols],
            send_sem=xsend.at[q], recv_sem=xrecv.at[q], device_id=mate, device_id_type=MESH)

    swaps = [swap(q) for q in range(nb // 2)]
    for s in swaps:
        s.start()

    def coords(k):
        return (b, a) if k % 2 == 0 else (a, b)

    def reduce_copies(k, s):
        first = k % 2 == 0
        me1, me2 = coords(k)
        big, small = 32 * (k + 1), 8 * (k + 1)
        base = panel_at(k)
        made = []
        for d in range(1, 4):
            if s == 0:
                at = pl.multiple_of(base + ((me1 + d) % 4) * big, 8)
                src, dst = gloc.at[pl.ds(at, big)], r1.at[d - 1, pl.ds(base // 4, big)]
                peer = along(first, d)
            elif s == 1:
                at = pl.multiple_of(base // 4 + ((me2 + d) % 4) * small, 8)
                src, dst = ysum.at[pl.ds(at, small)], r2.at[d - 1, pl.ds(base // 16, small)]
                peer = along(not first, d)
            elif s == 2:
                at = pl.multiple_of(base + me1 * big + me2 * small, 8)
                src = dst = gfull.at[pl.ds(at, small)]
                peer = along(not first, d)
            else:
                at = pl.multiple_of(base + me1 * big, 8)
                src = dst = gfull.at[pl.ds(at, big)]
                peer = along(first, d)
            made.append(pltpu.make_async_remote_copy(
                src_ref=src, dst_ref=dst, send_sem=asend.at[k, s, d - 1], recv_sem=arecv.at[k, s, d - 1],
                device_id={"row": peer}, device_id_type=MESH))
        return made

    copies = {}

    def begin(k, s):
        copies[k, s] = reduce_copies(k, s)
        for c in copies[k, s]:
            c.start()

    def event(k, s):
        me1, me2 = coords(k)
        big, small = 32 * (k + 1), 8 * (k + 1)
        base = panel_at(k)
        for c in copies[k, s - 1]:
            c.wait_recv()
        if s == 1:
            at = pl.multiple_of(base + me1 * big, 8)
            here = slice(base // 4, base // 4 + big)
            ysum[here, :] = (gloc[pl.ds(at, big), :] + r1[0, here, :]) + (r1[1, here, :] + r1[2, here, :])
            begin(k, 1)
        elif s == 2:
            at = pl.multiple_of(base // 4 + me2 * small, 8)
            here = slice(base // 16, base // 16 + small)
            to = pl.multiple_of(base + me1 * big + me2 * small, 8)
            gfull[pl.ds(to, small), :] = (ysum[pl.ds(at, small), :] + r2[0, here, :]) + (r2[1, here, :] + r2[2, here, :])
            begin(k, 2)
        elif s == 3:
            begin(k, 3)

    def wave(*pairs):
        for q, s in pairs:
            event(2 * q, s)
            event(2 * q + 1, s)

    for q in range(nb // 2):
        cols = slice(256 * q, 256 * q + 256)
        swaps[q].wait_recv()
        prod = part[core, :, cols] + pin[:, cols]
        hi, lo = halves(prod)
        phi[:, cols] = hi
        plo[:, cols] = lo
        turned = prod.T
        hi_t, lo_t = halves(turned)
        thi[cols, :] = hi_t
        tlo[cols, :] = lo_t
        n = 256 * q + 256
        for i in range(0, n, 256):
            ii = slice(i, i + 256)
            g = dot(thi[ii, :], hi) + (dot(tlo[ii, :], hi) + dot(thi[ii, :], lo))
            e = panel_at(2 * q)
            o = panel_at(2 * q + 1)
            take = min(256, e + 256 * q + B - (e + i))
            gloc[e + i : e + i + take, :] = g[:take, :B]
            gloc[o + i : o + i + 256, :] = g[:, B:]
        begin(2 * q, 0)
        begin(2 * q + 1, 0)

    wave((0, 1))
    wave((0, 2), (1, 1))
    wave((0, 3), (1, 2), (2, 1))
    wave((0, 4), (1, 3), (2, 2), (3, 1))

    out_copies = []
    for k in range(nb):
        base = panel_at(k)
        n = B * k
        kk = slice(n, n + B)
        block = gfull[base + n : base + n + B, :]
        if k > 0:
            ghi, glo = halves(gfull[base : base + n, :])
            gboth = jnp.concatenate([ghi, glo], axis=1)
            parts = []
            for i in range(k):
                m = B * i + B
                ii = slice(B * i, m)
                r = dot(whi[ii, :m], gboth[:m]) + dot(wlo[ii, :m], gboth[:m])
                parts.append(r[:, :B] + r[:, B:])
            r = jnp.concatenate(parts, axis=0)
            rhi, rlo = halves(r)
            rboth = jnp.concatenate([rhi, rlo], axis=1)
            thr, tlr = halves(r.T)
            d = dot(thr, rboth) + dot(tlr, rboth)
            block = block - (d[:, :B] + d[:, B:])
        inv = diag_inverse(block, work, winv)
        ihi, ilo = halves(inv)
        whi[kk, kk] = ihi
        wlo[kk, kk] = ilo
        if k > 0:
            t = dot(thr, whi[:n, :n]) + (dot(tlr, whi[:n, :n]) + dot(thr, wlo[:n, :n]))
            w = -dot(left_stack(inv), right_stack(t))
            hi, lo = halves(w)
            whi[kk, :n] = hi
            wlo[kk, :n] = lo
        if k + 1 < nb:
            for i in range(k + 1):
                zero = jnp.zeros((B, B), BF16)
                whi[B * i : B * i + B, n + B : n + 2 * B] = zero
                wlo[B * i : B * i + B, n + B : n + 2 * B] = zero
        m = n + B
        x[:, kk] = dot_t(phi[:, :m], whi[kk, :m]) + (dot_t(plo[:, :m], whi[kk, :m]) + dot_t(phi[:, :m], wlo[kk, :m]))
        if k % 2 == 1:
            cols = slice(n - B, n + B)
            c = pltpu.make_async_remote_copy(
                src_ref=x.at[pl.ds(pl.multiple_of((1 - core) * half, 8), half), cols],
                dst_ref=out.at[core, :, cols],
                send_sem=osend.at[k // 2], recv_sem=orecv.at[k // 2], device_id=mate, device_id_type=MESH)
            c.start()
            out_copies.append(c)
            out[core, :, cols] = x[pl.ds(pl.multiple_of(core * half, 8), half), cols]
        if k == 0:
            wave((1, 4), (2, 3), (3, 2))
        elif k == 2:
            wave((2, 4), (3, 3))
        elif k == 4:
            wave((3, 4))

    for c in out_copies:
        c.wait()
    for s in swaps:
        s.wait_send()
    for made in copies.values():
        for c in made:
            c.wait_send()


def refresh(part):
    _, rows, k = part.shape
    nb = k // B
    vm = pl.BlockSpec(memory_space=pltpu.VMEM)
    total = panel_at(nb)
    dma = pltpu.SemaphoreType.DMA
    return pl.pallas_call(
        functools.partial(kernel, nb),
        out_shape=jax.ShapeDtypeStruct((2, rows // 2, k), F32),
        in_specs=[vm],
        out_specs=vm,
        scratch_shapes=[
            pltpu.VMEM((rows, k), F32),
            pltpu.VMEM((rows, k), BF16),
            pltpu.VMEM((rows, k), BF16),
            pltpu.VMEM((k, rows), BF16),
            pltpu.VMEM((k, rows), BF16),
            pltpu.VMEM((total, B), F32),
            pltpu.VMEM((total, B), F32),
            pltpu.VMEM((total // 4, B), F32),
            pltpu.VMEM((3, total // 4, B), F32),
            pltpu.VMEM((3, total // 16, B), F32),
            pltpu.VMEM((k, k), BF16),
            pltpu.VMEM((k, k), BF16),
            pltpu.VMEM((rows, k), F32),
            pltpu.VMEM((B, B), F32),
            pltpu.VMEM((B, B), F32),
            dma((nb // 2,)),
            dma((nb // 2,)),
            dma((nb // 2,)),
            dma((nb // 2,)),
            dma((nb, 4, 3)),
            dma((nb, 4, 3)),
        ],
        compiler_params=pltpu.CompilerParams(
            vmem_limit_bytes=48 << 20, collective_id=0, has_side_effects=True),
        name="refresh",
    )(part)


def on_device(statistic, eigenbasis):
    part = lax.dot_general(
        statistic, eigenbasis, (((2,), (1,)), ((0,), (0,))), precision=HIGH, preferred_element_type=F32)
    return refresh(part)


def solution(mesh):
    placed = (P("layer", "row", "col"), P("layer", "col", None))
    return jax.shard_map(
        on_device,
        mesh=mesh,
        in_specs=placed,
        out_specs=P("layer", ("row", "col"), None),
        check_vma=False,
    )
```

time: 888 us -> 112 us (0.13)
  other arithmetic: 525 us -> 0 us
  waiting for transfers between devices: 130 us -> 0 us
  matrix products: 136 us -> 26.1 us
  Pallas kernels: 0 us -> 84.2 us
  local copies, waits for them, and re-layouts: 63.8 us -> 1.23 us
  between operations: 24 us -> 0.02 us
    another operation x68 -> x0, other arithmetic: 515 us -> none  [the longest x62 346 us: on_device(): factor = jnp.linalg.cholesky(gram_matrix)]
    psum x1 -> x0, waiting for transfers between devices: 122 us -> none  [on_device(): gram_matrix = lax.psum(contract(row_product, row_product), ('row', 'col'))]
    pallas_call x0 -> x1, Pallas kernels: none -> 84.2 us  [refresh(): pl.pallas_call(functools.partial(kernel, nb), out_shape=jax.ShapeDtypeStr...]
    another operation x58 -> x0, matrix products: 71.4 us -> none  [the longest x28 46.5 us: on_device(): factor = jnp.linalg.cholesky(gram_matrix)]
    another operation x67 -> x0, local copies, waits for them, and re-layouts: 51 us -> none  [the longest x51 45.1 us: on_device(): lax.linalg.triangular_solve(factor, row_product, left_side=False, lower=T...]
    dot_general x4 -> x1, matrix products: 64.4 us -> 26.1 us  [on_device(): lax.dot_general(statistic, eigenbasis, (((2,), (1,)), ((0,), (0,))), prec...]
    psum x2 -> x0, local copies, waits for them, and re-layouts: 10.9 us -> none  [on_device(): gram_matrix = lax.psum(contract(row_product, row_product), ('row', 'col'))]
    div x1 -> x0, other arithmetic: 10.3 us -> none  [on_device(): factor = jnp.linalg.cholesky(gram_matrix)]
  transfers between devices with their start and end apart: 3 -> 0, of which waited for: 2 -> 0; matrix products, arithmetic and copies ran while one was open for 4% -> 0% of each run, Pallas kernels for 0% -> 0%
where the time goes in v2:
time: 112 us
  Pallas kernels  84.2 us (75%)
  matrix products  26.1 us (23%)
  local copies, waits for them, and re-layouts  1.23 us (1%)
    pallas_call x1, Pallas kernels, refresh(): pl.pallas_call(functools.partial(kernel, nb), out_shape=jax.ShapeDtypeStr...  84.2 us
    dot_general x1, matrix products, on_device(): lax.dot_general(statistic, eigenbasis, (((2,), (1,)), ((0,), (0,))), prec...  26.1 us

profile of v2, /device:TPU:1, one launch (start us, length us, event | category | flops | bytes accessed | tf_op | source)
XLA Modules:
  0.0 111.6 jit_solution(1600165631896862921)
XLA Ops:
  0.0 26.1 %fusion.part = f32[2,448,1024]{2,1,0:T(8,128)S(1)} fusion(f32[2,448,3584]{2,1,0:T(8,128)} %param.2, f32[2,3584,1024]{2,1,0:T(8,128)} %param.3), kind=kOutput, calls=%fused_computation | convolution fusion | flops 19730006016 | bytes 45875200 | tf_op jit(solution)/shard_map/dot_general | solution.py:324
  26.1 84.2 %refresh.1 = f32[2,224,1024]{2,1,0:T(8,128)S(1)} custom-call(f32[2,448,1024]{2,1,0:T(8,128)S(1)} %fusion.part), custom_call_target="tpu_custom_call" | custom-call | tf_op jit(solution)/shard_map/refresh/pallas_call | solution.py:289
  110.3 1.2 %copy.4 = f32[2,224,1024]{2,1,0:T(8,128)} copy(f32[2,224,1024]{2,1,0:T(8,128)S(1)} %refresh.1) | data formatting | bytes 3670016

commit v3 on v2

--- a/solution.py
+++ b/solution.py
@@ -8,8 +8,8 @@
 
 F32, BF16 = jnp.float32, jnp.bfloat16
 MESH = pl.DeviceIdType.MESH
-HIGH = lax.Precision.HIGH
 B = 128
+KC = 512
 
 
 def halves(x):
@@ -93,8 +93,8 @@
     return B * k * (k + 1) // 2
 
 
-def kernel(nb, part, out, pin, phi, plo, thi, tlo, gloc, gfull, ysum, r1, r2, whi, wlo, x, work, winv,
-           xsend, xrecv, osend, orecv, asend, arecv):
+def kernel(nb, stat, basis, out, stage, shi, slo, bbuf, pacc, pin, phi, plo, thi, tlo, gloc, gfull, ysum, r1, r2,
+           whi, wlo, x, work, winv, ssem, bsem, xsend, xrecv, osend, orecv, asend, arecv):
     core = lax.axis_index("col")
     row = lax.axis_index("row")
     a, b = row // 4, row % 4
@@ -104,6 +104,29 @@
         if first:
             return a * 4 + (b + d) % 4
         return ((a + d) % 4) * 4 + b
+
+    rows = phi.shape[0]
+    half = rows // 2
+    depth = basis.shape[1]
+    nk = depth // KC
+
+    def layer_of(i):
+        return i * core + (1 - i) * (1 - core)
+
+    def stat_copy(i, kc):
+        ks = pl.ds(pl.multiple_of(kc * KC, 128), KC)
+        return pltpu.make_async_copy(stat.at[layer_of(i), :, ks], stage.at[kc], ssem.at[kc])
+
+    def basis_copy(i, q, kc, size):
+        ks = pl.ds(pl.multiple_of(kc * size, 128), size)
+        cols = pl.ds(pl.multiple_of(q * 256, 128), 256)
+        return pltpu.make_async_copy(basis.at[layer_of(i), ks, cols], bbuf.at[i, ks, :], bsem.at[i, kc])
+
+    for kc in range(nk):
+        stat_copy(0, kc).start()
+        basis_copy(0, 0, kc, KC).start()
+    for kc in range(nk):
+        basis_copy(1, 0, kc, KC).start()
 
     barrier = pltpu.get_barrier_semaphore()
     pl.semaphore_signal(barrier, inc=1, device_id=mate, device_id_type=MESH)
@@ -112,19 +135,10 @@
         pl.semaphore_signal(barrier, inc=1, device_id={"row": along(False, d)}, device_id_type=MESH)
     pl.semaphore_wait(barrier, 7)
 
-    rows = phi.shape[0]
-    half = rows // 2
-    sends = []
-
     def swap(q):
-        cols = slice(256 * q, 256 * q + 256)
         return pltpu.make_async_remote_copy(
-            src_ref=part.at[1 - core, :, cols], dst_ref=pin.at[:, cols],
+            src_ref=pacc.at[2 * q], dst_ref=pin.at[q],
             send_sem=xsend.at[q], recv_sem=xrecv.at[q], device_id=mate, device_id_type=MESH)
-
-    swaps = [swap(q) for q in range(nb // 2)]
-    for s in swaps:
-        s.start()
 
     def coords(k):
         return (b, a) if k % 2 == 0 else (a, b)
@@ -157,18 +171,15 @@
                 device_id={"row": peer}, device_id_type=MESH))
         return made
 
-    copies = {}
-
     def begin(k, s):
-        copies[k, s] = reduce_copies(k, s)
-        for c in copies[k, s]:
+        for c in reduce_copies(k, s):
             c.start()
 
     def event(k, s):
         me1, me2 = coords(k)
         big, small = 32 * (k + 1), 8 * (k + 1)
         base = panel_at(k)
-        for c in copies[k, s - 1]:
+        for c in reduce_copies(k, s - 1):
             c.wait_recv()
         if s == 1:
             at = pl.multiple_of(base + me1 * big, 8)
@@ -189,33 +200,92 @@
             event(2 * q, s)
             event(2 * q + 1, s)
 
-    for q in range(nb // 2):
+    def gram(q):
         cols = slice(256 * q, 256 * q + 256)
-        swaps[q].wait_recv()
-        prod = part[core, :, cols] + pin[:, cols]
+        swap(q).wait_recv()
+        prod = pacc[2 * q + 1] + pin[q]
         hi, lo = halves(prod)
         phi[:, cols] = hi
         plo[:, cols] = lo
-        turned = prod.T
-        hi_t, lo_t = halves(turned)
+        hi_t, lo_t = halves(prod.T)
         thi[cols, :] = hi_t
         tlo[cols, :] = lo_t
-        n = 256 * q + 256
-        for i in range(0, n, 256):
+        e, o = panel_at(2 * q), panel_at(2 * q + 1)
+        for i in range(0, 256 * q + 256, 256):
             ii = slice(i, i + 256)
             g = dot(thi[ii, :], hi) + (dot(tlo[ii, :], hi) + dot(thi[ii, :], lo))
-            e = panel_at(2 * q)
-            o = panel_at(2 * q + 1)
-            take = min(256, e + 256 * q + B - (e + i))
+            take = min(256, 256 * q + B - i)
             gloc[e + i : e + i + take, :] = g[:take, :B]
             gloc[o + i : o + i + 256, :] = g[:, B:]
         begin(2 * q, 0)
         begin(2 * q + 1, 0)
 
-    wave((0, 1))
-    wave((0, 2), (1, 1))
-    wave((0, 3), (1, 2), (2, 1))
-    wave((0, 4), (1, 3), (2, 2), (3, 1))
+    for i in range(2):
+
+        def first(kc, carry):
+            stat_copy(i, kc).wait()
+            basis_copy(i, 0, kc, KC).wait()
+            ks = pl.ds(pl.multiple_of(kc * KC, 128), KC)
+            hi, lo = halves(stage[kc])
+            shi[i, :, ks] = hi
+            slo[i, :, ks] = lo
+            if i == 0:
+                stat_copy(1, kc).start()
+            bhi, blo = halves(bbuf[i, ks, :])
+            r = dot(hi, bhi) + dot(lo, bhi) + dot(hi, blo)
+
+            @pl.when(kc == 0)
+            def _():
+                pacc[i] = r
+
+            @pl.when(kc > 0)
+            def _():
+                pacc[i] += r
+
+            return carry
+
+        lax.fori_loop(0, nk, first, 0)
+        for kc in range(2):
+            basis_copy(i, 1, kc, depth // 2).start()
+        if i == 0:
+            swap(0).start()
+    gram(0)
+
+    plan = {
+        2: ((0, 1),), 3: ((0, 2),), 4: ((0, 3), (1, 1)), 5: ((0, 4), (1, 2)), 6: ((1, 3), (2, 1)), 7: ((1, 4), (2, 2)),
+    }
+
+    def column_step(t, carry):
+        q, i = t // 2, t % 2
+        for kc in range(2):
+            basis_copy(i, q, kc, depth // 2).wait()
+        acc = None
+        for kc in range(2):
+            ks = slice(kc * depth // 2, (kc + 1) * depth // 2)
+            bhi, blo = halves(bbuf[i, ks, :])
+            for left, right in ((shi, bhi), (slo, bhi), (shi, blo)):
+                r = dot(left[i, :, ks], right)
+                acc = r if acc is None else acc + r
+        pacc[t] = acc
+
+        @pl.when(t < 6)
+        def _():
+            for kc in range(2):
+                basis_copy(i, q + 1, kc, depth // 2).start()
+
+        for tt in range(2, 8):
+
+            @pl.when(t == tt)
+            def _():
+                if tt % 2 == 0:
+                    swap(tt // 2).start()
+                wave(*plan[tt])
+                if tt % 2 == 1:
+                    gram(tt // 2)
+
+        return carry
+
+    lax.fori_loop(2, 8, column_step, 0)
 
     out_copies = []
     for k in range(nb):
@@ -264,24 +334,21 @@
             c.start()
             out_copies.append(c)
             out[core, :, cols] = x[pl.ds(pl.multiple_of(core * half, 8), half), cols]
-        if k == 0:
-            wave((1, 4), (2, 3), (3, 2))
-        elif k == 2:
-            wave((2, 4), (3, 3))
-        elif k == 4:
-            wave((3, 4))
+        wave(*{0: ((2, 3),), 1: ((2, 4), (3, 1)), 2: ((3, 2),), 3: ((3, 3),), 5: ((3, 4),)}.get(k, ()))
 
     for c in out_copies:
         c.wait()
-    for s in swaps:
-        s.wait_send()
-    for made in copies.values():
-        for c in made:
-            c.wait_send()
-
-
-def refresh(part):
-    _, rows, k = part.shape
+    for q in range(nb // 2):
+        swap(q).wait_send()
+    for k in range(nb):
+        for s in range(4):
+            for c in reduce_copies(k, s):
+                c.wait_send()
+
+
+def refresh(statistic, eigenbasis):
+    _, rows, depth = statistic.shape
+    k = eigenbasis.shape[2]
     nb = k // B
     vm = pl.BlockSpec(memory_space=pltpu.VMEM)
     total = panel_at(nb)
@@ -289,10 +356,15 @@
     return pl.pallas_call(
         functools.partial(kernel, nb),
         out_shape=jax.ShapeDtypeStruct((2, rows // 2, k), F32),
-        in_specs=[vm],
+        in_specs=[pl.BlockSpec(memory_space=pl.ANY)] * 2,
         out_specs=vm,
         scratch_shapes=[
-            pltpu.VMEM((rows, k), F32),
+            pltpu.VMEM((depth // KC, rows, KC), F32),
+            pltpu.VMEM((2, rows, depth), BF16),
+            pltpu.VMEM((2, rows, depth), BF16),
+            pltpu.VMEM((2, depth, 256), F32),
+            pltpu.VMEM((8, rows, 256), F32),
+            pltpu.VMEM((4, rows, 256), F32),
             pltpu.VMEM((rows, k), BF16),
             pltpu.VMEM((rows, k), BF16),
             pltpu.VMEM((k, rows), BF16),
@@ -307,6 +379,8 @@
             pltpu.VMEM((rows, k), F32),
             pltpu.VMEM((B, B), F32),
             pltpu.VMEM((B, B), F32),
+            dma((depth // KC,)),
+            dma((2, depth // KC)),
             dma((nb // 2,)),
             dma((nb // 2,)),
             dma((nb // 2,)),
@@ -315,21 +389,15 @@
             dma((nb, 4, 3)),
         ],
         compiler_params=pltpu.CompilerParams(
-            vmem_limit_bytes=48 << 20, collective_id=0, has_side_effects=True),
+            vmem_limit_bytes=67043328, collective_id=0, has_side_effects=True),
         name="refresh",
-    )(part)
-
-
-def on_device(statistic, eigenbasis):
-    part = lax.dot_general(
-        statistic, eigenbasis, (((2,), (1,)), ((0,), (0,))), precision=HIGH, preferred_element_type=F32)
-    return refresh(part)
+    )(statistic, eigenbasis)
 
 
 def solution(mesh):
     placed = (P("layer", "row", "col"), P("layer", "col", None))
     return jax.shard_map(
-        on_device,
+        refresh,
         mesh=mesh,
         in_specs=placed,
         out_specs=P("layer", ("row", "col"), None),

time: 112 us -> 101 us (0.902)
  matrix products: 26.1 us -> 0 us
  Pallas kernels: 84.2 us -> 97.6 us
  local copies, waits for them, and re-layouts: 1.23 us -> 2.94 us
    dot_general x1 -> x0, matrix products: 26.1 us -> none  [on_device(): lax.dot_general(statistic, eigenbasis, (((2,), (1,)), ((0,), (0,))), prec...]
    pallas_call x1, Pallas kernels: 84.2 us -> 97.6 us  [refresh(): pl.pallas_call(functools.partial(kernel, nb), out_shape=jax.ShapeDtypeStr...]
    unnamed x1, local copies, waits for them, and re-layouts: 1.23 us -> 2.94 us
where the time goes in v3:
time: 101 us
  Pallas kernels  97.6 us (97%)
  local copies, waits for them, and re-layouts  2.94 us (3%)
    pallas_call x1, Pallas kernels, refresh(): pl.pallas_call(functools.partial(kernel, nb), out_shape=jax.ShapeDtypeStr...  97.6 us
    unnamed x1, local copies, waits for them, and re-layouts  2.94 us

profile of v3, /device:TPU:1, one launch (start us, length us, event | category | flops | bytes accessed | tf_op | source)
XLA Modules:
  0.0 100.6 jit_solution(4957084229355277694)
XLA Ops:
  0.0 97.6 %refresh.1 = f32[2,224,1024]{2,1,0:T(8,128)} custom-call(f32[2,448,3584]{2,1,0:T(8,128)} %stat.1, f32[2,3584,1024]{2,1,0:T(8,128)} %basis.1), custom_call_target="tpu_custom_call" | custom-call | tf_op jit(solution)/shard_map/refresh/pallas_call | solution.py:356
  97.7 2.9 %copy.4 = f32[2,224,1024]{2,1,0:T(8,128)} copy(f32[2,224,1024]{2,1,0:T(8,128)} %refresh.1) | data formatting | bytes 3670016

commit v4 on v3

--- a/solution.py
+++ b/solution.py
@@ -36,47 +36,56 @@
     return jnp.concatenate([hi, hi, lo, lo], axis=0)
 
 
-def factor_group(rows, inv, col0):
+def spread(v, s):
+    return jnp.broadcast_to(v[s : s + 1, :], (8, 128))
+
+
+def factor_group(rows, inv, col0, wide):
     n = len(rows)
     sub = lax.broadcasted_iota(jnp.int32, (8, 128), 0)
-    for t in range(n):
+    for t in range(0, n, wide // 8):
         base = col0 + 8 * t
-        cols = [
-            [jnp.broadcast_to(rows[g][:, base + j : base + j + 1], (8, 128)) for g in range(t, n)]
-            for j in range(8)
-        ]
+        cols = []
+        for j in range(wide):
+            col = {}
+            for g in range(t + j // 8, n):
+                c = jnp.broadcast_to(rows[g][:, base + j : base + j + 1], (8, 128))
+                col[g] = c + 0.0 if g < t + wide // 8 else c
+            cols.append(col)
+        pivot = spread(cols[0][t], 0)
         scale = None
-        for j in range(8):
-            pivot = jnp.broadcast_to(cols[j][0][j : j + 1, :], (8, 128))
-            recip = 1.0 / pivot
+        for j in range(wide):
+            gj, s = t + j // 8, j % 8
+            mult = {g: c / pivot for g, c in cols[j].items()}
+            across = {k: spread(cols[j][t + k // 8], k % 8) for k in range(j + 1, wide)}
             rs = lax.rsqrt(pivot)
-            scale = rs if scale is None else jnp.where(sub >= j, rs, scale)
-            mult = [c * recip for c in cols[j]]
-            mult[0] = jnp.where(sub > j, mult[0], 0.0)
-            for k in range(j + 1, 8):
-                across = jnp.broadcast_to(cols[k][0][j : j + 1, :], (8, 128))
-                cols[k] = [c - m * across for c, m in zip(cols[k], mult)]
-            row = jnp.broadcast_to(rows[t][j : j + 1, :], (8, 128))
-            irow = jnp.broadcast_to(inv[t][j : j + 1, :], (8, 128))
-            for g in range(t, n):
-                rows[g] = rows[g] - mult[g - t] * row
-                inv[g] = inv[g] - mult[g - t] * irow
-        rows[t] = rows[t] * scale
-        inv[t] = inv[t] * scale
+            scale = rs if s == 0 else jnp.where(sub >= s, rs, scale)
+            if j + 1 < wide:
+                own = spread(cols[j + 1][t + (j + 1) // 8], (j + 1) % 8)
+                pivot = own - (across[j + 1] * across[j + 1]) / pivot
+            for k in range(j + 1, wide):
+                for g in cols[k]:
+                    cols[k][g] = cols[k][g] - mult[g] * across[k]
+            mult[gj] = jnp.where(sub > s, mult[gj], 0.0)
+            row, irow = spread(rows[gj], s), spread(inv[gj], s)
+            for g in mult:
+                rows[g] = rows[g] - mult[g] * row
+                inv[g] = inv[g] - mult[g] * irow
+            if s == 7:
+                rows[gj] = rows[gj] * scale
+                inv[gj] = inv[gj] * scale
     return rows, inv
 
 
-def diag_inverse(block, work, winv):
+def diag_inverse(block, work, winv, step=64, wide=16):
     r = lax.broadcasted_iota(jnp.int32, (B, B), 0)
     c = lax.broadcasted_iota(jnp.int32, (B, B), 1)
     work[...] = block
     winv[...] = jnp.where(r == c, 1.0, 0.0).astype(F32)
-    step = 32
-    for q in range(B // step):
-        lo = q * step
+    for lo in range(0, B, step):
         rows = [work[lo + 8 * g : lo + 8 * g + 8, :] for g in range(step // 8)]
         inv = [winv[lo + 8 * g : lo + 8 * g + 8, :] for g in range(step // 8)]
-        rows, inv = factor_group(rows, inv, lo)
+        rows, inv = factor_group(rows, inv, lo, wide)
         rfull = jnp.concatenate(rows, axis=0)
         ifull = jnp.concatenate(inv, axis=0)
         winv[lo : lo + step, :] = ifull
@@ -93,7 +102,7 @@
     return B * k * (k + 1) // 2
 
 
-def kernel(nb, stat, basis, out, stage, shi, slo, bbuf, pacc, pin, phi, plo, thi, tlo, gloc, gfull, ysum, r1, r2,
+def kernel(nb, stat, basis, out, stage, shi, slo, bbuf, pacc, pin, phi, plo, thi, tlo, gloc, gfull, ysum, rh, r1, r2,
            whi, wlo, x, work, winv, ssem, bsem, xsend, xrecv, osend, orecv, asend, arecv):
     core = lax.axis_index("col")
     row = lax.axis_index("row")
@@ -147,28 +156,42 @@
         first = k % 2 == 0
         me1, me2 = coords(k)
         big, small = 32 * (k + 1), 8 * (k + 1)
+        part = big // 2
         base = panel_at(k)
+
+        def rows_of(chunk, size, shift=0):
+            return pl.ds(pl.multiple_of(base + chunk % 4 * big + shift, 8), size)
+
         made = []
-        for d in range(1, 4):
+
+        def add(src, dst, peer):
+            d = len(made)
+            made.append(pltpu.make_async_remote_copy(
+                src_ref=src, dst_ref=dst, send_sem=asend.at[k, s, d], recv_sem=arecv.at[k, s, d],
+                device_id={"row": peer}, device_id_type=MESH))
+
+        if s in (2, 3):
+            for d in range(1, 4):
+                if s == 2:
+                    at = pl.multiple_of(base // 4 + ((me2 + d) % 4) * small, 8)
+                    src, dst = ysum.at[pl.ds(at, small)], r2.at[d - 1, pl.ds(base // 16, small)]
+                else:
+                    at = pl.multiple_of(base + me1 * big + me2 * small, 8)
+                    src = dst = gfull.at[pl.ds(at, small)]
+                add(src, dst, along(not first, d))
+            return made
+        for way, d in enumerate((1, 3)):
             if s == 0:
-                at = pl.multiple_of(base + ((me1 + d) % 4) * big, 8)
-                src, dst = gloc.at[pl.ds(at, big)], r1.at[d - 1, pl.ds(base // 4, big)]
-                peer = along(first, d)
+                src = gloc.at[rows_of(me1 + 2, part, way * part)]
+                dst = rh.at[way, pl.ds(base // 8, part)]
             elif s == 1:
-                at = pl.multiple_of(base // 4 + ((me2 + d) % 4) * small, 8)
-                src, dst = ysum.at[pl.ds(at, small)], r2.at[d - 1, pl.ds(base // 16, small)]
-                peer = along(not first, d)
-            elif s == 2:
-                at = pl.multiple_of(base + me1 * big + me2 * small, 8)
-                src = dst = gfull.at[pl.ds(at, small)]
-                peer = along(not first, d)
+                src = gloc.at[rows_of(me1 + d, big)]
+                dst = r1.at[way, pl.ds(base // 4, big)]
+            elif s == 4:
+                src = dst = gfull.at[rows_of(me1, big)]
             else:
-                at = pl.multiple_of(base + me1 * big, 8)
-                src = dst = gfull.at[pl.ds(at, big)]
-                peer = along(first, d)
-            made.append(pltpu.make_async_remote_copy(
-                src_ref=src, dst_ref=dst, send_sem=asend.at[k, s, d - 1], recv_sem=arecv.at[k, s, d - 1],
-                device_id={"row": peer}, device_id_type=MESH))
+                src = dst = gfull.at[rows_of(me1 + 4 - d, part, way * part)]
+            add(src, dst, along(first, d))
         return made
 
     def begin(k, s):
@@ -182,18 +205,21 @@
         for c in reduce_copies(k, s - 1):
             c.wait_recv()
         if s == 1:
+            part = big // 2
+            for way, d in enumerate((1, 3)):
+                at = pl.multiple_of(base + (me1 + d) % 4 * big + way * part, 8)
+                gloc[pl.ds(at, part), :] += rh[way, base // 8 : base // 8 + part, :]
+        elif s == 2:
             at = pl.multiple_of(base + me1 * big, 8)
             here = slice(base // 4, base // 4 + big)
-            ysum[here, :] = (gloc[pl.ds(at, big), :] + r1[0, here, :]) + (r1[1, here, :] + r1[2, here, :])
-            begin(k, 1)
-        elif s == 2:
+            ysum[here, :] = gloc[pl.ds(at, big), :] + (r1[0, here, :] + r1[1, here, :])
+        elif s == 3:
             at = pl.multiple_of(base // 4 + me2 * small, 8)
             here = slice(base // 16, base // 16 + small)
             to = pl.multiple_of(base + me1 * big + me2 * small, 8)
             gfull[pl.ds(to, small), :] = (ysum[pl.ds(at, small), :] + r2[0, here, :]) + (r2[1, here, :] + r2[2, here, :])
-            begin(k, 2)
-        elif s == 3:
-            begin(k, 3)
+        if s < 6:
+            begin(k, s)
 
     def wave(*pairs):
         for q, s in pairs:
@@ -252,7 +278,8 @@
     gram(0)
 
     plan = {
-        2: ((0, 1),), 3: ((0, 2),), 4: ((0, 3), (1, 1)), 5: ((0, 4), (1, 2)), 6: ((1, 3), (2, 1)), 7: ((1, 4), (2, 2)),
+        2: ((0, 1),), 3: ((0, 2),), 4: ((0, 3), (1, 1)), 5: ((0, 4), (1, 2)),
+        6: ((0, 5), (1, 3), (2, 1)), 7: ((0, 6), (1, 4), (2, 2)),
     }
 
     def column_step(t, carry):
@@ -287,6 +314,10 @@
 
     lax.fori_loop(2, 8, column_step, 0)
 
+    late = {
+        0: ((1, 5), (2, 3), (3, 1)), 1: ((1, 6), (2, 4), (3, 2)), 2: ((2, 5), (3, 3)), 3: ((2, 6), (3, 4)),
+        4: ((3, 5),), 5: ((3, 6),),
+    }
     out_copies = []
     for k in range(nb):
         base = panel_at(k)
@@ -334,14 +365,14 @@
             c.start()
             out_copies.append(c)
             out[core, :, cols] = x[pl.ds(pl.multiple_of(core * half, 8), half), cols]
-        wave(*{0: ((2, 3),), 1: ((2, 4), (3, 1)), 2: ((3, 2),), 3: ((3, 3),), 5: ((3, 4),)}.get(k, ()))
+        wave(*late.get(k, ()))
 
     for c in out_copies:
         c.wait()
     for q in range(nb // 2):
         swap(q).wait_send()
     for k in range(nb):
-        for s in range(4):
+        for s in range(6):
             for c in reduce_copies(k, s):
                 c.wait_send()
 
@@ -372,7 +403,8 @@
             pltpu.VMEM((total, B), F32),
             pltpu.VMEM((total, B), F32),
             pltpu.VMEM((total // 4, B), F32),
-            pltpu.VMEM((3, total // 4, B), F32),
+            pltpu.VMEM((2, total // 8, B), F32),
+            pltpu.VMEM((2, total // 4, B), F32),
             pltpu.VMEM((3, total // 16, B), F32),
             pltpu.VMEM((k, k), BF16),
             pltpu.VMEM((k, k), BF16),
@@ -385,8 +417,8 @@
             dma((nb // 2,)),
             dma((nb // 2,)),
             dma((nb // 2,)),
-            dma((nb, 4, 3)),
-            dma((nb, 4, 3)),
+            dma((nb, 6, 3)),
+            dma((nb, 6, 3)),
         ],
         compiler_params=pltpu.CompilerParams(
             vmem_limit_bytes=67043328, collective_id=0, has_side_effects=True),

time: 101 us -> 88.6 us (0.88)
  Pallas kernels: 97.6 us -> 85.6 us
    pallas_call x1, Pallas kernels: 97.6 us -> 85.6 us  [refresh(): pl.pallas_call(functools.partial(kernel, nb), out_shape=jax.ShapeDtypeStr...]
where the time goes in v4:
time: 88.6 us; the launch traced here: 88.5 us
  Pallas kernels  85.6 us (97%)
  local copies, waits for them, and re-layouts  2.94 us (3%)
    pallas_call x1, Pallas kernels, refresh(): pl.pallas_call(functools.partial(kernel, nb), out_shape=jax.ShapeDtypeStr...  85.6 us
    unnamed x1, local copies, waits for them, and re-layouts  2.94 us

profile of v4, /device:TPU:1, one launch (start us, length us, event | category | flops | bytes accessed | tf_op | source)
XLA Modules:
  0.0 88.5 jit_solution(2381984896203017143)
XLA Ops:
  0.0 85.6 %refresh.1 = f32[2,224,1024]{2,1,0:T(8,128)} custom-call(f32[2,448,3584]{2,1,0:T(8,128)} %stat.1, f32[2,3584,1024]{2,1,0:T(8,128)} %basis.1), custom_call_target="tpu_custom_call" | custom-call | tf_op jit(solution)/shard_map/refresh/pallas_call | solution.py:387
  85.6 2.9 %copy.4 = f32[2,224,1024]{2,1,0:T(8,128)} copy(f32[2,224,1024]{2,1,0:T(8,128)} %refresh.1) | data formatting | bytes 3670016

commit v5 on v4

--- a/solution.py
+++ b/solution.py
@@ -10,6 +10,14 @@
 MESH = pl.DeviceIdType.MESH
 B = 128
 KC = 512
+RING = (2, 3)
+LATE = (4, 6)
+DIRECT_STAGES = ("all", "second", "spread2", "spread")
+RING_STAGES = ("half", "whole", "second", "spread2", "near", "relay")
+
+
+def stages(k):
+    return RING_STAGES if k // 2 in RING else DIRECT_STAGES
 
 
 def halves(x):
@@ -40,7 +48,7 @@
     return jnp.broadcast_to(v[s : s + 1, :], (8, 128))
 
 
-def factor_group(rows, inv, col0, wide):
+def factor_group(rows, inv, col0, wide, fill):
     n = len(rows)
     sub = lax.broadcasted_iota(jnp.int32, (8, 128), 0)
     for t in range(0, n, wide // 8):
@@ -74,10 +82,11 @@
             if s == 7:
                 rows[gj] = rows[gj] * scale
                 inv[gj] = inv[gj] * scale
+            fill()
     return rows, inv
 
 
-def diag_inverse(block, work, winv, step=64, wide=16):
+def diag_inverse(block, work, winv, fill, step=64, wide=16):
     r = lax.broadcasted_iota(jnp.int32, (B, B), 0)
     c = lax.broadcasted_iota(jnp.int32, (B, B), 1)
     work[...] = block
@@ -85,7 +94,7 @@
     for lo in range(0, B, step):
         rows = [work[lo + 8 * g : lo + 8 * g + 8, :] for g in range(step // 8)]
         inv = [winv[lo + 8 * g : lo + 8 * g + 8, :] for g in range(step // 8)]
-        rows, inv = factor_group(rows, inv, lo, wide)
+        rows, inv = factor_group(rows, inv, lo, wide, fill)
         rfull = jnp.concatenate(rows, axis=0)
         ifull = jnp.concatenate(inv, axis=0)
         winv[lo : lo + step, :] = ifull
@@ -102,8 +111,130 @@
     return B * k * (k + 1) // 2
 
 
+def factor_and_solve(nb, gfull, phi, plo, whi, wlo, x, work, winv, gboth, rboth, thr, tlr, tk, bd, after):
+    rows = phi.shape[0]
+    zero = jnp.zeros((B, B), BF16)
+    for i in range(0, nb, 2):
+        whi[B * i : B * i + B, B * i + B : B * i + 2 * B] = zero
+        wlo[B * i : B * i + B, B * i + B : B * i + 2 * B] = zero
+
+    def block(i, k):
+        at = panel_at(k) + B * i
+        return gfull[at : at + B, :]
+
+    def against(side, other, n):
+        d = dot(thr[side, :, :n], rboth[other, :n, :]) + dot(tlr[side, :, :n], rboth[other, :n, :])
+        return d[:, :B] + d[:, B:]
+
+    def keep_r(side, i, r):
+        ii = slice(B * i, B * i + B)
+        hi, lo = halves(r)
+        rboth[side, ii, :B] = hi
+        rboth[side, ii, B:] = lo
+        hi, lo = halves(r.T)
+        thr[side, :, ii] = hi
+        tlr[side, :, ii] = lo
+
+    def row_of_w(k):
+        ii = slice(B * k, B * k + B)
+
+        def chunk(c, e):
+            mh, ml = whi[ii, ii], wlo[ii, ii]
+            th, tl = tk[0, :, c:e], tk[1, :, c:e]
+            w = dot(jnp.concatenate([mh, ml], axis=1), jnp.concatenate([th, th], axis=0)) + dot(
+                jnp.concatenate([mh, ml], axis=1), jnp.concatenate([tl, tl], axis=0))
+            hi, lo = halves(-w)
+            whi[ii, c:e] = hi
+            wlo[ii, c:e] = lo
+
+        return [functools.partial(chunk, c, min(c + 256, B * k)) for c in range(0, B * k, 256)]
+
+    def t_of(k):
+        n = B * k
+
+        def chunk(c, e):
+            th, tl = thr[k % 2, :, c:n], tlr[k % 2, :, c:n]
+            t = dot(th, whi[c:n, c:e]) + (dot(tl, whi[c:n, c:e]) + dot(th, wlo[c:n, c:e]))
+            hi, lo = halves(t)
+            tk[0, :, c:e] = hi
+            tk[1, :, c:e] = lo
+
+        return [functools.partial(chunk, c, min(c + 256, n)) for c in range(0, n, 256)]
+
+    def x_of(k):
+        kk, m = slice(B * k, B * k + B), B * k + B
+
+        def chunk(c):
+            r = slice(c, c + rows // 4)
+            x[r, kk] = dot_t(phi[r, :m], whi[kk, :m]) + (dot_t(plo[r, :m], whi[kk, :m]) + dot_t(phi[r, :m], wlo[kk, :m]))
+
+        return [functools.partial(chunk, c) for c in range(0, rows, rows // 4)]
+
+    def r_of(k):
+        side, n = k % 2, B * (k - 1)
+
+        def split():
+            at = panel_at(k)
+            hi, lo = halves(gfull[at : at + n, :])
+            gboth[:n, :B] = hi
+            gboth[:n, B:] = lo
+
+        def one(i):
+            ii, m = slice(B * i, B * i + B), B * i + B
+            r = dot(whi[ii, :m], gboth[:m, :]) + dot(wlo[ii, :m], gboth[:m, :])
+            keep_r(side, i, r[:, :B] + r[:, B:])
+
+        def rest():
+            b, d = block(k - 1, k), block(k, k)
+            if n:
+                b = b - against(1 - side, side, n)
+                d = d - against(side, side, n)
+            bd[0] = b
+            bd[1] = d
+
+        return ([split] if n else []) + [functools.partial(one, i) for i in range(k - 1)] + [rest]
+
+    current = block(0, 0)
+    for k in range(nb):
+        jobs = []
+        if k > 0:
+            jobs += row_of_w(k - 1) + t_of(k)
+        if k + 1 < nb and k + 1 not in LATE:
+            jobs += r_of(k + 1)
+        if k > 0:
+            jobs += x_of(k - 1)
+        every = max(1, 112 // (len(jobs) + 1))
+        count = [0]
+
+        def fill():
+            count[0] += 1
+            if count[0] % every == 0 and jobs:
+                jobs.pop(0)()
+
+        inv = diag_inverse(current, work, winv, fill)
+        while jobs:
+            jobs.pop(0)()
+        kk = slice(B * k, B * k + B)
+        hi, lo = halves(inv)
+        whi[kk, kk] = hi
+        wlo[kk, kk] = lo
+        if k + 1 in LATE:
+            after(k)
+            for job in r_of(k + 1):
+                job()
+        if k + 1 < nb:
+            side = (k + 1) % 2
+            keep_r(side, k, dot(left_stack(inv), right_stack(bd[0])))
+            d = dot(thr[side, :, kk], rboth[side, kk, :]) + dot(tlr[side, :, kk], rboth[side, kk, :])
+            current = bd[1] - (d[:, :B] + d[:, B:])
+        if k + 1 not in LATE:
+            after(k)
+    for job in row_of_w(nb - 1) + x_of(nb - 1):
+        job()
+
+
 def kernel(nb, stat, basis, out, stage, shi, slo, bbuf, pacc, pin, phi, plo, thi, tlo, gloc, gfull, ysum, rh, r1, r2,
-           whi, wlo, x, work, winv, ssem, bsem, xsend, xrecv, osend, orecv, asend, arecv):
+           whi, wlo, x, work, winv, gboth, rboth, thr, tlr, tk, bd, ssem, bsem, xsend, xrecv, osend, orecv, asend, arecv):
     core = lax.axis_index("col")
     row = lax.axis_index("row")
     a, b = row // 4, row % 4
@@ -153,6 +284,7 @@
         return (b, a) if k % 2 == 0 else (a, b)
 
     def reduce_copies(k, s):
+        kind = stages(k)[s]
         first = k % 2 == 0
         me1, me2 = coords(k)
         big, small = 32 * (k + 1), 8 * (k + 1)
@@ -163,35 +295,29 @@
             return pl.ds(pl.multiple_of(base + chunk % 4 * big + shift, 8), size)
 
         made = []
-
-        def add(src, dst, peer):
-            d = len(made)
-            made.append(pltpu.make_async_remote_copy(
-                src_ref=src, dst_ref=dst, send_sem=asend.at[k, s, d], recv_sem=arecv.at[k, s, d],
-                device_id={"row": peer}, device_id_type=MESH))
-
-        if s in (2, 3):
-            for d in range(1, 4):
-                if s == 2:
-                    at = pl.multiple_of(base // 4 + ((me2 + d) % 4) * small, 8)
-                    src, dst = ysum.at[pl.ds(at, small)], r2.at[d - 1, pl.ds(base // 16, small)]
-                else:
-                    at = pl.multiple_of(base + me1 * big + me2 * small, 8)
-                    src = dst = gfull.at[pl.ds(at, small)]
-                add(src, dst, along(not first, d))
-            return made
-        for way, d in enumerate((1, 3)):
-            if s == 0:
-                src = gloc.at[rows_of(me1 + 2, part, way * part)]
-                dst = rh.at[way, pl.ds(base // 8, part)]
-            elif s == 1:
-                src = gloc.at[rows_of(me1 + d, big)]
-                dst = r1.at[way, pl.ds(base // 4, big)]
-            elif s == 4:
+        for n, d in enumerate((1, 2, 3) if kind in ("all", "second", "spread2", "spread") else (1, 3)):
+            peer = along(first, d)
+            if kind == "all":
+                src, dst = gloc.at[rows_of(me1 + d, big)], r1.at[n, pl.ds(base // 4, big)]
+            elif kind == "half":
+                src, dst = gloc.at[rows_of(me1 + 2, part, n * part)], rh.at[n, pl.ds(base // 8, part)]
+            elif kind == "whole":
+                src, dst = gloc.at[rows_of(me1 + d, big)], r1.at[n, pl.ds(base // 4, big)]
+            elif kind == "second":
+                at = pl.multiple_of(base // 4 + ((me2 + d) % 4) * small, 8)
+                src, dst = ysum.at[pl.ds(at, small)], r2.at[n, pl.ds(base // 16, small)]
+                peer = along(not first, d)
+            elif kind == "spread2":
+                at = pl.multiple_of(base + me1 * big + me2 * small, 8)
+                src = dst = gfull.at[pl.ds(at, small)]
+                peer = along(not first, d)
+            elif kind in ("spread", "near"):
                 src = dst = gfull.at[rows_of(me1, big)]
             else:
-                src = dst = gfull.at[rows_of(me1 + 4 - d, part, way * part)]
-            add(src, dst, along(first, d))
+                src = dst = gfull.at[rows_of(me1 + 4 - d, part, n * part)]
+            made.append(pltpu.make_async_remote_copy(
+                src_ref=src, dst_ref=dst, send_sem=asend.at[k, s, n], recv_sem=arecv.at[k, s, n],
+                device_id={"row": peer}, device_id_type=MESH))
         return made
 
     def begin(k, s):
@@ -204,21 +330,23 @@
         base = panel_at(k)
         for c in reduce_copies(k, s - 1):
             c.wait_recv()
-        if s == 1:
+        done = stages(k)[s - 1]
+        if done == "half":
             part = big // 2
             for way, d in enumerate((1, 3)):
                 at = pl.multiple_of(base + (me1 + d) % 4 * big + way * part, 8)
                 gloc[pl.ds(at, part), :] += rh[way, base // 8 : base // 8 + part, :]
-        elif s == 2:
+        elif done in ("all", "whole"):
             at = pl.multiple_of(base + me1 * big, 8)
             here = slice(base // 4, base // 4 + big)
-            ysum[here, :] = gloc[pl.ds(at, big), :] + (r1[0, here, :] + r1[1, here, :])
-        elif s == 3:
+            total = gloc[pl.ds(at, big), :] + (r1[0, here, :] + r1[1, here, :])
+            ysum[here, :] = total + r1[2, here, :] if done == "all" else total
+        elif done == "second":
             at = pl.multiple_of(base // 4 + me2 * small, 8)
             here = slice(base // 16, base // 16 + small)
             to = pl.multiple_of(base + me1 * big + me2 * small, 8)
             gfull[pl.ds(to, small), :] = (ysum[pl.ds(at, small), :] + r2[0, here, :]) + (r2[1, here, :] + r2[2, here, :])
-        if s < 6:
+        if s < len(stages(k)):
             begin(k, s)
 
     def wave(*pairs):
@@ -277,10 +405,7 @@
             swap(0).start()
     gram(0)
 
-    plan = {
-        2: ((0, 1),), 3: ((0, 2),), 4: ((0, 3), (1, 1)), 5: ((0, 4), (1, 2)),
-        6: ((0, 5), (1, 3), (2, 1)), 7: ((0, 6), (1, 4), (2, 2)),
-    }
+    plan = {3: ((0, 1),), 4: ((0, 2),), 5: ((0, 3), (1, 1)), 6: ((1, 2), (2, 1)), 7: ((0, 4), (1, 3), (2, 2))}
 
     def column_step(t, carry):
         q, i = t // 2, t % 2
@@ -306,7 +431,7 @@
             def _():
                 if tt % 2 == 0:
                     swap(tt // 2).start()
-                wave(*plan[tt])
+                wave(*plan.get(tt, ()))
                 if tt % 2 == 1:
                     gram(tt // 2)
 
@@ -315,64 +440,34 @@
     lax.fori_loop(2, 8, column_step, 0)
 
     late = {
-        0: ((1, 5), (2, 3), (3, 1)), 1: ((1, 6), (2, 4), (3, 2)), 2: ((2, 5), (3, 3)), 3: ((2, 6), (3, 4)),
-        4: ((3, 5),), 5: ((3, 6),),
+        0: ((1, 4), (2, 3), (3, 1)), 1: ((2, 4), (3, 2)), 2: ((2, 5), (3, 3)), 3: ((2, 6), (3, 4)), 4: ((3, 5),), 5: ((3, 6),),
     }
     out_copies = []
-    for k in range(nb):
-        base = panel_at(k)
-        n = B * k
-        kk = slice(n, n + B)
-        block = gfull[base + n : base + n + B, :]
-        if k > 0:
-            ghi, glo = halves(gfull[base : base + n, :])
-            gboth = jnp.concatenate([ghi, glo], axis=1)
-            parts = []
-            for i in range(k):
-                m = B * i + B
-                ii = slice(B * i, m)
-                r = dot(whi[ii, :m], gboth[:m]) + dot(wlo[ii, :m], gboth[:m])
-                parts.append(r[:, :B] + r[:, B:])
-            r = jnp.concatenate(parts, axis=0)
-            rhi, rlo = halves(r)
-            rboth = jnp.concatenate([rhi, rlo], axis=1)
-            thr, tlr = halves(r.T)
-            d = dot(thr, rboth) + dot(tlr, rboth)
-            block = block - (d[:, :B] + d[:, B:])
-        inv = diag_inverse(block, work, winv)
-        ihi, ilo = halves(inv)
-        whi[kk, kk] = ihi
-        wlo[kk, kk] = ilo
-        if k > 0:
-            t = dot(thr, whi[:n, :n]) + (dot(tlr, whi[:n, :n]) + dot(thr, wlo[:n, :n]))
-            w = -dot(left_stack(inv), right_stack(t))
-            hi, lo = halves(w)
-            whi[kk, :n] = hi
-            wlo[kk, :n] = lo
-        if k + 1 < nb:
-            for i in range(k + 1):
-                zero = jnp.zeros((B, B), BF16)
-                whi[B * i : B * i + B, n + B : n + 2 * B] = zero
-                wlo[B * i : B * i + B, n + B : n + 2 * B] = zero
-        m = n + B
-        x[:, kk] = dot_t(phi[:, :m], whi[kk, :m]) + (dot_t(plo[:, :m], whi[kk, :m]) + dot_t(phi[:, :m], wlo[kk, :m]))
-        if k % 2 == 1:
-            cols = slice(n - B, n + B)
-            c = pltpu.make_async_remote_copy(
-                src_ref=x.at[pl.ds(pl.multiple_of((1 - core) * half, 8), half), cols],
-                dst_ref=out.at[core, :, cols],
-                send_sem=osend.at[k // 2], recv_sem=orecv.at[k // 2], device_id=mate, device_id_type=MESH)
-            c.start()
-            out_copies.append(c)
-            out[core, :, cols] = x[pl.ds(pl.multiple_of(core * half, 8), half), cols]
+
+    def give(q):
+        cols = slice(256 * q, 256 * q + 256)
+        c = pltpu.make_async_remote_copy(
+            src_ref=x.at[pl.ds(pl.multiple_of((1 - core) * half, 8), half), cols],
+            dst_ref=out.at[core, :, cols],
+            send_sem=osend.at[q], recv_sem=orecv.at[q], device_id=mate, device_id_type=MESH)
+        c.start()
+        out_copies.append(c)
+        out[core, :, cols] = x[pl.ds(pl.multiple_of(core * half, 8), half), cols]
+
+    def after(k):
         wave(*late.get(k, ()))
+        if k > 0 and k % 2 == 0:
+            give(k // 2 - 1)
+
+    factor_and_solve(nb, gfull, phi, plo, whi, wlo, x, work, winv, gboth, rboth, thr, tlr, tk, bd, after)
+    give(nb // 2 - 1)
 
     for c in out_copies:
         c.wait()
     for q in range(nb // 2):
         swap(q).wait_send()
     for k in range(nb):
-        for s in range(6):
+        for s in range(len(stages(k))):
             for c in reduce_copies(k, s):
                 c.wait_send()
 
@@ -404,13 +499,19 @@
             pltpu.VMEM((total, B), F32),
             pltpu.VMEM((total // 4, B), F32),
             pltpu.VMEM((2, total // 8, B), F32),
-            pltpu.VMEM((2, total // 4, B), F32),
+            pltpu.VMEM((3, total // 4, B), F32),
             pltpu.VMEM((3, total // 16, B), F32),
             pltpu.VMEM((k, k), BF16),
             pltpu.VMEM((k, k), BF16),
             pltpu.VMEM((rows, k), F32),
             pltpu.VMEM((B, B), F32),
             pltpu.VMEM((B, B), F32),
+            pltpu.VMEM((k, 2 * B), BF16),
+            pltpu.VMEM((2, k, 2 * B), BF16),
+            pltpu.VMEM((2, B, k), BF16),
+            pltpu.VMEM((2, B, k), BF16),
+            pltpu.VMEM((2, B, k), BF16),
+            pltpu.VMEM((2, B, B), F32),
             dma((depth // KC,)),
             dma((2, depth // KC)),
             dma((nb // 2,)),

time: 88.6 us -> 84.4 us (0.953)
  Pallas kernels: 85.6 us -> 81.3 us
    pallas_call x1, Pallas kernels: 85.6 us -> 81.3 us  [refresh(): pl.pallas_call(functools.partial(kernel, nb), out_shape=jax.ShapeDtypeStr...]
where the time goes in v5:
time: 84.4 us; the launch traced here: 84.3 us
  Pallas kernels  81.3 us (96%)
  local copies, waits for them, and re-layouts  2.94 us (3%)
    pallas_call x1, Pallas kernels, refresh(): pl.pallas_call(functools.partial(kernel, nb), out_shape=jax.ShapeDtypeStr...  81.3 us
    unnamed x1, local copies, waits for them, and re-layouts  2.94 us

profile of v5, /device:TPU:1, one launch (start us, length us, event | category | flops | bytes accessed | tf_op | source)
XLA Modules:
  0.0 84.3 jit_solution(13766835249006704475)
XLA Ops:
  0.0 81.3 %refresh.1 = f32[2,224,1024]{2,1,0:T(8,128)} custom-call(f32[2,448,3584]{2,1,0:T(8,128)} %stat.1, f32[2,3584,1024]{2,1,0:T(8,128)} %basis.1), custom_call_target="tpu_custom_call" | custom-call | tf_op jit(solution)/shard_map/refresh/pallas_call | solution.py:482
  81.3 2.9 %copy.4 = f32[2,224,1024]{2,1,0:T(8,128)} copy(f32[2,224,1024]{2,1,0:T(8,128)} %refresh.1) | data formatting | bytes 3670016

commit v6 on v5

--- a/solution.py
+++ b/solution.py
@@ -234,7 +234,7 @@
 
 
 def kernel(nb, stat, basis, out, stage, shi, slo, bbuf, pacc, pin, phi, plo, thi, tlo, gloc, gfull, ysum, rh, r1, r2,
-           whi, wlo, x, work, winv, gboth, rboth, thr, tlr, tk, bd, ssem, bsem, xsend, xrecv, osend, orecv, asend, arecv):
+           whi, wlo, x, work, winv, gboth, rboth, thr, tlr, tk, bd, ssem, bsem, xsend, xrecv, osend, orecv, olocal, asend, arecv):
     core = lax.axis_index("col")
     row = lax.axis_index("row")
     a, b = row // 4, row % 4
@@ -273,7 +273,6 @@
     for d in range(1, 4):
         pl.semaphore_signal(barrier, inc=1, device_id={"row": along(True, d)}, device_id_type=MESH)
         pl.semaphore_signal(barrier, inc=1, device_id={"row": along(False, d)}, device_id_type=MESH)
-    pl.semaphore_wait(barrier, 7)
 
     def swap(q):
         return pltpu.make_async_remote_copy(
@@ -402,6 +401,7 @@
         for kc in range(2):
             basis_copy(i, 1, kc, depth // 2).start()
         if i == 0:
+            pl.semaphore_wait(barrier, 7)
             swap(0).start()
     gram(0)
 
@@ -440,27 +440,31 @@
     lax.fori_loop(2, 8, column_step, 0)
 
     late = {
-        0: ((1, 4), (2, 3), (3, 1)), 1: ((2, 4), (3, 2)), 2: ((2, 5), (3, 3)), 3: ((2, 6), (3, 4)), 4: ((3, 5),), 5: ((3, 6),),
+        0: ((3, 1), (2, 3), (1, 4)), 1: ((3, 2), (2, 4)), 2: ((3, 3), (2, 5)), 3: ((3, 4), (2, 6)), 4: ((3, 5),), 5: ((3, 6),),
     }
     out_copies = []
 
-    def give(q):
-        cols = slice(256 * q, 256 * q + 256)
-        c = pltpu.make_async_remote_copy(
+    def give(n, cols):
+        theirs = pltpu.make_async_remote_copy(
             src_ref=x.at[pl.ds(pl.multiple_of((1 - core) * half, 8), half), cols],
             dst_ref=out.at[core, :, cols],
-            send_sem=osend.at[q], recv_sem=orecv.at[q], device_id=mate, device_id_type=MESH)
-        c.start()
-        out_copies.append(c)
-        out[core, :, cols] = x[pl.ds(pl.multiple_of(core * half, 8), half), cols]
+            send_sem=osend.at[n], recv_sem=orecv.at[n], device_id=mate, device_id_type=MESH)
+        ours = pltpu.make_async_copy(
+            x.at[pl.ds(pl.multiple_of(core * half, 8), half), cols], out.at[core, :, cols], olocal.at[n])
+        theirs.start()
+        ours.start()
+        out_copies.append(theirs)
+        out_copies.append(ours)
 
     def after(k):
         wave(*late.get(k, ()))
         if k > 0 and k % 2 == 0:
-            give(k // 2 - 1)
+            give(k // 2 - 1, slice(B * (k - 2), B * k))
+        if k == nb - 1:
+            give(nb // 2 - 1, slice(B * (k - 1), B * k))
 
     factor_and_solve(nb, gfull, phi, plo, whi, wlo, x, work, winv, gboth, rboth, thr, tlr, tk, bd, after)
-    give(nb // 2 - 1)
+    give(nb // 2, slice(B * (nb - 1), B * nb))
 
     for c in out_copies:
         c.wait()
@@ -476,14 +480,13 @@
     _, rows, depth = statistic.shape
     k = eigenbasis.shape[2]
     nb = k // B
-    vm = pl.BlockSpec(memory_space=pltpu.VMEM)
     total = panel_at(nb)
     dma = pltpu.SemaphoreType.DMA
     return pl.pallas_call(
         functools.partial(kernel, nb),
         out_shape=jax.ShapeDtypeStruct((2, rows // 2, k), F32),
         in_specs=[pl.BlockSpec(memory_space=pl.ANY)] * 2,
-        out_specs=vm,
+        out_specs=pl.BlockSpec(memory_space=pl.ANY),
         scratch_shapes=[
             pltpu.VMEM((depth // KC, rows, KC), F32),
             pltpu.VMEM((2, rows, depth), BF16),
@@ -516,8 +519,9 @@
             dma((2, depth // KC)),
             dma((nb // 2,)),
             dma((nb // 2,)),
-            dma((nb // 2,)),
-            dma((nb // 2,)),
+            dma((nb // 2 + 1,)),
+            dma((nb // 2 + 1,)),
+            dma((nb // 2 + 1,)),
             dma((nb, 6, 3)),
             dma((nb, 6, 3)),
         ],

time: 84.4 us -> 83.7 us (level)
  no operation moved by 1% of the time
where the time goes in v6:
time: 83.7 us; the launch traced here: 83.5 us
  Pallas kernels  80.6 us (96%)
  local copies, waits for them, and re-layouts  2.94 us (4%)
    pallas_call x1, Pallas kernels, refresh(): pl.pallas_call(functools.partial(kernel, nb), out_shape=jax.ShapeDtypeStr...  80.6 us
    unnamed x1, local copies, waits for them, and re-layouts  2.94 us

profile of v6, /device:TPU:1, one launch (start us, length us, event | category | flops | bytes accessed | tf_op | source)
XLA Modules:
  0.0 83.5 jit_solution(393485182210889787)
XLA Ops:
  0.0 80.6 %refresh.1 = f32[2,224,1024]{2,1,0:T(8,128)} custom-call(f32[2,448,3584]{2,1,0:T(8,128)} %stat.1, f32[2,3584,1024]{2,1,0:T(8,128)} %basis.1), custom_call_target="tpu_custom_call" | custom-call | tf_op jit(solution)/shard_map/refresh/pallas_call | solution.py:485
  80.6 2.9 %copy.4 = f32[2,224,1024]{2,1,0:T(8,128)} copy(f32[2,224,1024]{2,1,0:T(8,128)} %refresh.1) | data formatting | bytes 3670016

commit v7 on v6

--- a/solution.py
+++ b/solution.py
@@ -9,7 +9,7 @@
 F32, BF16 = jnp.float32, jnp.bfloat16
 MESH = pl.DeviceIdType.MESH
 B = 128
-KC = 512
+KC = 1792
 RING = (2, 3)
 LATE = (4, 6)
 DIRECT_STAGES = ("all", "second", "spread2", "spread")

time: 83.7 us -> 82.2 us (0.982)
  Pallas kernels: 80.6 us -> 79.1 us
    pallas_call x1, Pallas kernels: 80.6 us -> 79.1 us  [refresh(): pl.pallas_call(functools.partial(kernel, nb), out_shape=jax.ShapeDtypeStr...]
where the time goes in v7:
time: 82.2 us; the launch traced here: 82 us
  Pallas kernels  79.1 us (96%)
  local copies, waits for them, and re-layouts  2.94 us (4%)
    pallas_call x1, Pallas kernels, refresh(): pl.pallas_call(functools.partial(kernel, nb), out_shape=jax.ShapeDtypeStr...  79.1 us
    unnamed x1, local copies, waits for them, and re-layouts  2.94 us

profile of v7, /device:TPU:1, one launch (start us, length us, event | category | flops | bytes accessed | tf_op | source)
XLA Modules:
  0.0 82.0 jit_solution(9571673806240051313)
XLA Ops:
  0.0 79.1 %refresh.1 = f32[2,224,1024]{2,1,0:T(8,128)} custom-call(f32[2,448,3584]{2,1,0:T(8,128)} %stat.1, f32[2,3584,1024]{2,1,0:T(8,128)} %basis.1), custom_call_target="tpu_custom_call" | custom-call | tf_op jit(solution)/shard_map/refresh/pallas_call | solution.py:485
  79.1 2.9 %copy.4 = f32[2,224,1024]{2,1,0:T(8,128)} copy(f32[2,224,1024]{2,1,0:T(8,128)} %refresh.1) | data formatting | bytes 3670016
